TPU v7x, 512 devices: a whole 4x8x8 slice. The times are simulated.
512 devices in a mesh: expert: 64 (over z_lo, y, x), shard: 8 (over z_hi, core).
Axes of the slice: x: 4, y: 8, z: 8 (z_hi: 4, z_lo: 2; z = z_hi * 2 + z_lo), core: 2. Of those that a mesh axis runs over, the one named last changes fastest.
Arguments:
- w_gate: float32 [64, 2048, 1024], P('expert', 'shard'), may hold values from -0.125 to 0.125
- avg_gate: float32 [64, 2048, 1024], P('expert', 'shard'), may hold values from -0.125 to 0.125
- w_up: float32 [64, 2048, 1024], P('expert', 'shard'), may hold values from -0.125 to 0.125
- avg_up: float32 [64, 2048, 1024], P('expert', 'shard'), may hold values from -0.125 to 0.125
- mix_share: float32 [64], P('expert'), may hold values from 0.2 to 0.8
- router_weight: float32 [2048, 64], P('shard', 'expert'), may hold values from -0.125 to 0.125
- router_gain: float32 [2048], P('shard'), may hold values from 0.25 to 1.75
Outputs:
- serve_gate: bfloat16 [64, 1024, 2048], P('expert')
- serve_up: bfloat16 [64, 1024, 2048], P('expert')
- serve_router: bfloat16 [2048, 64], replicated
All inputs are finite; a program needn't handle non-finite values.
Results may differ from a plain program's by a relative error of at most 0.001.
Values may be sent and summed in bfloat16 or wider, within the bound.
No kernel may reach another device: no remote copies, remote signals or barrier semaphores. Data moves between devices by JAX's collectives and lax.ppermute only.
A program may use at most 64 MiB of HBM per device.

v0:
```python
import jax
import jax.numpy as jnp
from jax import lax
from jax.sharding import PartitionSpec as P


def sent_together(arrays, axis, dim, along):
    ends, at = ([], 0)
    for a in arrays[:-1]:
        at += a.shape[along]
        ends.append(at)
    both = jnp.concatenate(arrays, axis=along)
    return tuple(jnp.split(lax.all_gather(both, axis, axis=dim, tiled=True), ends, axis=along))


def joined_along(parts, dim):
    parts = jnp.moveaxis(parts, 0, dim)
    lengths = parts.shape
    return parts.reshape(*lengths[:dim], lengths[dim] * lengths[dim + 1], *lengths[dim + 2 :])


def sent_to_all(x, axis):
    length = lax.axis_size(axis)
    return lax.all_to_all(jnp.broadcast_to(x[None], (length, *x.shape)), axis, 0, 0, tiled=True)


def gathered_copies(x, axis, dim):
    return joined_along(sent_to_all(x, axis), dim)


def local(w_gate, avg_gate, w_up, avg_up, mix_share, router_weight, router_gain):
    fresh_gate = mix_share[:, None, None] * w_gate + (1.0 - mix_share[:, None, None]) * avg_gate
    fresh_up = mix_share[:, None, None] * w_up + (1.0 - mix_share[:, None, None]) * avg_up
    narrow_gate, narrow_up = (fresh_gate.astype(jnp.bfloat16), fresh_up.astype(jnp.bfloat16))
    serve_gate, serve_up = sent_together((narrow_gate, narrow_up), "shard", 1, 0)
    serve_gate = jnp.transpose(serve_gate, (0, 2, 1))
    serve_up = jnp.transpose(serve_up, (0, 2, 1))
    part_router = (router_weight * router_gain[:, None]).astype(jnp.bfloat16)
    row_router = gathered_copies(part_router, "shard", 0)
    serve_router = gathered_copies(row_router, "expert", 1)
    return (serve_gate, serve_up, serve_router)


def solution(mesh):
    return jax.shard_map(
        local,
        mesh=mesh,
        in_specs=(
            P("expert", "shard", None),
            P("expert", "shard", None),
            P("expert", "shard", None),
            P("expert", "shard", None),
            P("expert"),
            P("shard", "expert"),
            P("shard"),
        ),
        out_specs=(P("expert", None, None), P("expert", None, None), P()),
        check_vma=False,
    )
```

profile of v0, /device:TPU:1, one launch (start us, length us, event | category | flops | bytes accessed | tf_op | source)
XLA Modules:
  0.0 134.6 jit_solution(16616703295714073848)
XLA Ops:
  7.2 0.0 all-gather.2.cloned.1.call-start
  7.9 1.6 %copy.22 = f32[1,256,1024]{1,2,0:T(8,128)S(1)} copy(f32[1,256,1024]{2,1,0:T(8,128)} %param.7) | data formatting | bytes 2097152 | tf_op args[0]
  9.4 1.6 %copy.23 = f32[1,256,1024]{1,2,0:T(8,128)S(1)} copy(f32[1,256,1024]{2,1,0:T(8,128)} %param.8) | data formatting | bytes 2097152 | tf_op args[1]
  11.0 1.6 %copy.24 = f32[1,256,1024]{1,2,0:T(8,128)S(1)} copy(f32[1,256,1024]{2,1,0:T(8,128)} %param.9) | data formatting | bytes 2097152 | tf_op args[2]
  12.5 2.5 %copy.25 = f32[1,256,1024]{1,2,0:T(8,128)} copy(f32[1,256,1024]{2,1,0:T(8,128)} %param.10) | data formatting | bytes 2097152 | tf_op args[3]
  15.1 0.0 copy-start
  15.1 0.0 copy-start.1
  15.1 1.6 %add_convert_fusion = (bf16[1,256,1024]{1,2,0:T(8,128)(2,1)S(1)}, bf16[1,256,1024]{1,2,0:T(8,128)(2,1)S(1)}) fusion(f32[1,256,1024]{1,2,0:T(8,128)} %copy.25, f32[1,256,1024]{1,2,0:T(8,128)S(1)} %copy.24, f32[]{:T(128)} %bitcast.1, f32[]{:T(128)} %bitcast.21, f32[1,256,1024]{1,2,0:T(8,128)S(1)} %copy.23, f32[1,256,1024]{1,2,0:T(8,128)S(1)} %copy.22), kind=kLoop, calls=%fused_computation.3 | loop fusion | flops 2097152 | bytes 5242888 | tf_op jit(solution)/shard_map/convert_element_type | solution.py:34
  16.6 1.1 pad_maximum_fusion
  17.7 0.0 all-gather.2.cloned.1.call-update
  17.7 0.0 copy-done
  17.7 0.0 copy-done.1
  17.8 0.5 broadcast.6
  18.3 0.7 reduce.4
  19.0 18.6 %all_to_all.10 = bf16[8,2,128]{2,1,0:T(2,128)(2,1)S(1)} all-to-all(bf16[8,2,128]{2,1,0:T(2,128)(2,1)S(1)} %reshape.26), channel_id=1, replica_groups=mesh['expert'=64,'shard'=8] {'shard'}, dimensions={0} | all-to-all | bytes 8192 | tf_op jit(solution)/shard_map/all_to_all | solution.py:24
  37.7 0.3 broadcast_bitcast_fusion
  37.9 2.2 %reduce.5 = bf16[64,2048]{1,0:T(8,128)(2,1)S(1)} reduce(bf16[64,1,2048]{2,1,0:T(2,128)(2,1)S(1)} %broadcast_bitcast_fusion, bf16[]{:T(256)} %broadcast.6), dimensions={1}, to_apply=%broadcast_bitcast_fusion.reduce_sub_computation | reduce | bytes 524290
  40.1 0.2 reshape.28
  40.3 26.6 %all_to_all.11 = bf16[64,2,1024]{2,1,0:T(2,128)(2,1)S(1)} all-to-all(bf16[64,2,1024]{2,1,0:T(2,128)(2,1)S(1)} %reshape.28), channel_id=1, replica_groups=mesh['expert'=64,'shard'=8] {'expert'}, dimensions={0} | all-to-all | bytes 524288 | tf_op jit(solution)/shard_map/all_to_all | solution.py:24
  66.9 0.2 reshape.29
  67.2 0.9 copy.29
  68.0 53.6 %all-gather.2.cloned.1.call-done = bf16[2,2048,1024]{1,2,0:T(8,128)(2,1)} async-done(((bf16[2,256,1024]{1,2,0:T(8,128)(2,1)}), bf16[2,2048,1024]{1,2,0:T(8,128)(2,1)}) %all-gather.2.cloned.1.call-update) | async-done | bytes 8388624 | tf_op jit(solution)/shard_map/all_gather | solution.py:13
  121.6 6.1 %slice_bitcast_fusion = (bf16[1,1024,2048]{2,1,0:T(8,128)(2,1)}, bf16[1,1024,2048]{2,1,0:T(8,128)(2,1)}) fusion(bf16[2,2048,1024]{1,2,0:T(8,128)(2,1)} %all-gather.2.cloned.1.call-done), kind=kLoop, calls=%fused_computation | loop fusion | bytes 16777216 | tf_op jit(solution)/shard_map/transpose | solution.py:37
  (6 shorter events, 0.1 us)
Async XLA Ops:
  7.2 114.5 %all-gather.2.cloned.1.call-start = ((), (), s32[]{:S(2)}) async-start(), calls=%async_computation.2 | async-start | bytes 9437184 | tf_op jit(solution)/shard_map/all_gather | solution.py:13
  15.1 2.6 %copy-start = (f32[256,1]{0,1:T(1,128)S(1)}, f32[256,1]{0,1:T(1,128)}, u32[]{:S(2)}) copy-start(f32[256,1]{0,1:T(1,128)} %param.12) | copy-start | bytes 3076
  15.1 2.7 %copy-start.1 = (f32[256]{0:T(256)S(1)}, f32[256]{0:T(256)}, u32[]{:S(2)}) copy-start(f32[256]{0:T(256)} %param.13) | copy-start | bytes 3076
Sparse Core Ops, SparseCore 0:
  17.8 103.7 all-gather.1
where the time goes:
time: 135 us
  waiting for transfers between devices  53.6 us (40%)
  blocking collectives  45.3 us (34%)
  local copies, waits for them, and re-layouts  15.5 us (11%)
  between operations  14.8 us (11%)
  other arithmetic  5.48 us (4%)
    all_gather x1, waiting for transfers between devices, sent_together(): lax.all_gather(both, axis, axis=dim, tiled=True)  53.6 us
    all_to_all x2, blocking collectives, sent_to_all(): lax.all_to_all(jnp.broadcast_to(x[None], (length, *x.shape)), axis, 0, 0,...  45.3 us
    unnamed x16, local copies, waits for them, and re-layouts  8.44 us
    transpose x1, local copies, waits for them, and re-layouts, local(): serve_up = jnp.transpose(serve_up, (0, 2, 1))  6.14 us
    unnamed x2, other arithmetic  2.84 us
  transfers between devices with their start and end apart: 1, of which 1 were waited for; matrix products, arithmetic and copies ran while one was open for 4% of the time, Pallas kernels for 0%

commit v1 on v0

v1 whole, which is shorter than its diff:
```python
import functools

import jax
import jax.numpy as jnp
from jax import lax
from jax.experimental import pallas as pl
from jax.experimental.pallas import tpu as pltpu
from jax.sharding import Mesh
from jax.sharding import PartitionSpec as P


BF16 = jnp.bfloat16
PIECES = 4
EXPERT = ("zlo", "y", "x")
SHARD = ("zhi", "core")
ANY = pl.BlockSpec(memory_space=pl.ANY)
HBM = pl.BlockSpec(memory_space=pltpu.HBM)
VMEM = pl.BlockSpec(memory_space=pltpu.VMEM)
SMEM = pl.BlockSpec(memory_space=pltpu.SMEM)
GATE, UP = 0, 1


def mix_kernel(share_ref, w_ref, avg_ref, *refs):
    before, outs, (buf, sems) = refs[:-4], refs[-4:-2], refs[-2:]
    rows = w_ref.shape[1]
    width = rows // PIECES

    def copies(piece):
        cols = pl.ds(piece * width, width)
        return [
            pltpu.make_async_copy(src.at[:, cols], buf.at[i, piece], sems.at[i, piece])
            for i, src in enumerate((w_ref, avg_ref))
        ]

    for piece in range(PIECES):
        for c in copies(piece):
            c.start()
    share = share_ref[0]
    rest = 1.0 - share
    for piece in range(PIECES):
        for c in copies(piece):
            c.wait()
        fresh = share * buf[0, piece] + rest * buf[1, piece]
        turned = fresh.T.astype(BF16)
        outs[0][pl.ds(piece * width, width), :] = turned
        if before:
            outs[1][pl.ds(piece * width, width), :] = before[0][pl.ds(piece * width, width), :]
            outs[1][pl.ds(rows + piece * width, width), :] = turned


def first_kernel(share_ref, w_ref, avg_ref, out_ref, buf, sems):
    mix_kernel(share_ref, w_ref, avg_ref, out_ref, None, buf, sems)


def mixed(share, w, avg, before=None):
    rows, cols = w.shape
    w, avg = (pltpu.with_memory_space_constraint(x, pltpu.HBM) for x in (w, avg))
    extra = () if before is None else (pltpu.with_memory_space_constraint(before, pltpu.VMEM),)
    return pl.pallas_call(
        mix_kernel if extra else first_kernel,
        out_shape=(pltpu.VMEM((cols, rows), BF16),) + ((pltpu.VMEM((2 * cols, rows), BF16),) if extra else ()),
        in_specs=[SMEM, HBM, HBM] + [VMEM] * len(extra),
        out_specs=(VMEM,) * (1 + len(extra)),
        scratch_shapes=[
            pltpu.VMEM((2, PIECES, rows, cols // PIECES), jnp.float32),
            pltpu.SemaphoreType.DMA((2, PIECES)),
        ],
        compiler_params=pltpu.CompilerParams(vmem_limit_bytes=12 << 20),
        cost_estimate=pl.CostEstimate(flops=4 * rows * cols, bytes_accessed=10 * rows * cols, transcendentals=0),
        name="mix",
    )(share, w, avg, *extra)


def place_kernel(counts, by, join, *refs):
    outs, sems = refs[-3 - join : -1 - join], refs[-1]
    joined = refs[-2] if join else None
    width = refs[0].shape[1]
    chips = lax.axis_size("zhi")
    chip, core = lax.axis_index("zhi"), lax.axis_index("core")
    sign = 1 - 2 * lax.axis_index("zlo")
    copies, pieces, at = [], [], 0
    entries = iter(by)
    for ref, count in zip(refs, counts):
        row = 0
        for _ in range(count):
            which, start, size, step, other = next(entries)
            owner = lax.rem(chip + chips - step * sign, chips) * 2 + (1 - core if other else core)
            cols = pl.ds(pl.multiple_of(owner * width, width), width)
            piece = ref.at[pl.ds(row, size), :]
            row += size
            pieces.append((piece, size))
            copies.append(pltpu.make_async_copy(piece, outs[which].at[pl.ds(start, size), cols], sems.at[len(copies)]))
    for c in copies:
        c.start()
    if join:
        for piece, size in pieces:
            joined[pl.ds(at, size), :] = piece[...]
            at += size
    for c in copies:
        c.wait()


def placed(outs, arrays, columns, rows, join=False):
    n = len(arrays)
    by = tuple(p for _, pieces in arrays for p in pieces)
    counts = tuple(len(pieces) for _, pieces in arrays)
    arrays = [pltpu.with_memory_space_constraint(a, pltpu.VMEM) for a, _ in arrays]
    width = arrays[0].shape[1]
    total = sum(p[2] for p in by)
    out = jax.ShapeDtypeStruct((rows, columns), BF16)
    extra = () if outs is None else tuple(outs)
    res = pl.pallas_call(
        functools.partial(place_kernel, counts, by, int(join)),
        out_shape=(out, out) + ((pltpu.VMEM((total, width), BF16),) if join else ()),
        in_specs=[VMEM] * n + [ANY] * len(extra),
        out_specs=(ANY, ANY) + ((VMEM,) if join else ()),
        input_output_aliases={n + i: i for i in range(len(extra))},
        scratch_shapes=[pltpu.SemaphoreType.DMA((len(by),))],
        compiler_params=pltpu.CompilerParams(vmem_limit_bytes=12 << 20),
        cost_estimate=pl.CostEstimate(flops=2 * total * width, bytes_accessed=4 * total * width, transcendentals=0),
        name="place",
    )(*arrays, *extra)
    return res[:2], (res[2] if join else None)


def order_kernel(nx, ny, nz, in_ref, out_ref, wide, turned):
    lanes = in_ref.shape[1]
    wide[...] = in_ref[...].astype(jnp.float32)
    shards = in_ref.shape[0] // (nx * ny * nz * 2)
    for x in range(nx):
        for z in range(nz):
            for s in range(shards):
                for h in range(2):
                    rows = wide[pl.ds(((x * nz + z) * shards + s) * ny * 2 + h, ny, stride=2), :]
                    turned[s * 2 + h, pl.ds(z * ny * nx + x, ny, stride=nx), :] = rows
    for j in range(2 * shards):
        out_ref[:, pl.ds(j * lanes, lanes)] = turned[j].astype(BF16)


def ordered(part, nx, ny, nz):
    rows, lanes = part.shape
    experts = nx * ny * nz
    return pl.pallas_call(
        functools.partial(order_kernel, nx, ny, nz),
        out_shape=jax.ShapeDtypeStruct((experts, rows * lanes // experts), BF16),
        in_specs=[VMEM],
        out_specs=VMEM,
        scratch_shapes=[
            pltpu.VMEM((rows, lanes), jnp.float32),
            pltpu.VMEM((rows // experts, experts, lanes), jnp.float32),
        ],
        compiler_params=pltpu.CompilerParams(vmem_limit_bytes=4 << 20),
        cost_estimate=pl.CostEstimate(flops=rows * lanes, bytes_accessed=4 * rows * lanes, transcendentals=0),
        name="order",
    )(part)


def spread(x, axes):
    n = lax.axis_size(axes)
    return lax.all_to_all(jnp.broadcast_to(x[None], (n, *x.shape)), axes, 0, 0, tiled=True)


def local(w_gate, avg_gate, w_up, avg_up, mix_share, router_weight, router_gain):
    chips = lax.axis_size("zhi")
    columns = w_gate.shape[1] * chips * lax.axis_size("core")
    rows = w_gate.shape[2]

    def moved(x, by):
        pairs = [
            (lo * chips + hi, lo * chips + (hi + (by if lo == 0 else -by)) % chips) for lo in range(2) for hi in range(chips)
        ]
        return lax.ppermute(x, ("zlo", "zhi"), pairs)

    def partner(x):
        return lax.ppermute(x, "core", [(0, 1), (1, 0)])

    def place(outs, *arrays, join=False):
        return placed(outs, arrays, columns, rows, join)

    def pieces(step, other, *which):
        return tuple((w, 0, rows, step, other) for w in which)

    (gate,) = mixed(mix_share, w_gate[0], avg_gate[0])
    up, own = mixed(mix_share, w_up[0], avg_up[0], gate)
    a1 = moved(gate, 1)
    a2 = moved(up, 1)
    c1 = moved(a1, 1)
    c2 = moved(a2, 1)
    b1 = moved(gate, -1)
    b2 = moved(up, -1)

    nx, ny, nz = (lax.axis_size(a) for a in ("x", "y", "zlo"))
    part = (router_weight * router_gain[:, None]).astype(BF16).reshape(2, -1)
    lanes = part.shape[1]
    part = spread(part, ("y",)).reshape(-1, lanes)
    part = spread(part, ("zlo", "zhi", "core")).reshape(-1, lanes)
    part = spread(part, ("x",)).reshape(-1, lanes)
    serve_router = ordered(part, nx, ny, nz).T

    outs, _ = place(None, (own, pieces(0, 0, GATE, UP)))
    outs, _ = place(outs, (partner(own), pieces(0, 1, GATE, UP)))
    outs, both = place(outs, (a1, pieces(1, 0, GATE)), (a2, pieces(1, 0, UP)), join=True)
    outs, _ = place(outs, (partner(both), pieces(1, 1, GATE, UP)))
    c1_other = partner(c1)
    b1_other = partner(b1)
    b2_other = partner(b2)
    c2_other = partner(c2)
    outs, _ = place(outs, (c1, pieces(2, 0, GATE)), (c1_other, pieces(2, 1, GATE)), (b1, pieces(-1, 0, GATE)))
    outs, _ = place(outs, (b1_other, pieces(-1, 1, GATE)), (b2, pieces(-1, 0, UP)), (c2, pieces(2, 0, UP)))
    outs, _ = place(outs, (b2_other, pieces(-1, 1, UP)), (c2_other, pieces(2, 1, UP)))
    return outs[0][None], outs[1][None], serve_router


def solution(mesh):
    devices = mesh.devices.reshape(2, 8, 4, 4, 2)
    split = Mesh(devices, EXPERT + SHARD)
    return jax.shard_map(
        local,
        mesh=split,
        in_specs=(
            P(EXPERT, SHARD, None),
            P(EXPERT, SHARD, None),
            P(EXPERT, SHARD, None),
            P(EXPERT, SHARD, None),
            P(EXPERT),
            P(SHARD, EXPERT),
            P(SHARD),
        ),
        out_specs=(P(EXPERT, None, None), P(EXPERT, None, None), P()),
        check_vma=False,
    )
```

time: 135 us -> 145 us (1.074)
  starting transfers between devices: 0.04 us -> 42.5 us
  local copies, waits for them, and re-layouts: 15.5 us -> 0.06 us
  between operations: 14.8 us -> 1.52 us
  Pallas kernels: 0 us -> 11.6 us
  blocking collectives: 45.3 us -> 38.2 us
  other arithmetic: 5.48 us -> 0.02 us
  waiting for transfers between devices: 53.6 us -> 50.3 us
    all_gather x1 -> x0, waiting for transfers between devices: 53.6 us -> none  [sent_together(): lax.all_gather(both, axis, axis=dim, tiled=True)]
    ppermute x0 -> x12, waiting for transfers between devices: none -> 50.3 us  [the longest x6 50.3 us: moved(): return lax.ppermute(x, ('zlo', 'zhi'), pairs)]
    ppermute x0 -> x12, starting transfers between devices: none -> 42.5 us  [the longest x6 21.5 us: partner(): return lax.ppermute(x, 'core', [(0, 1), (1, 0)])]
    pallas_call x0 -> x10, Pallas kernels: none -> 11.6 us  [the longest x7 7.37 us: placed(): pl.pallas_call(functools.partial(place_kernel, counts, by, int(join)), ou...]
    unnamed x16 -> x4, local copies, waits for them, and re-layouts: 8.44 us -> 0.01 us
    all_to_all x2 -> x3, blocking collectives: 45.3 us -> 38.2 us  [spread(): lax.all_to_all(jnp.broadcast_to(x[None], (n, *x.shape)), axes, 0, 0, tile...]
    transpose x1 -> x0, local copies, waits for them, and re-layouts: 6.14 us -> none  [local(): serve_up = jnp.transpose(serve_up, (0, 2, 1))]
    unnamed x2 -> x0, other arithmetic: 2.84 us -> none
  transfers between devices with their start and end apart: 1 -> 12, of which waited for: 1 -> 5; matrix products, arithmetic and copies ran while one was open for 4% -> 0% of each run, Pallas kernels for 0% -> 4%
where the time goes in v1:
time: 145 us; the launch traced here: 144 us
  waiting for transfers between devices  50.3 us (35%)
  starting transfers between devices  42.5 us (29%)
  blocking collectives  38.2 us (26%)
  Pallas kernels  11.6 us (8%)
  between operations  1.52 us (1%)
    ppermute x6, waiting for transfers between devices, moved(): return lax.ppermute(x, ('zlo', 'zhi'), pairs)  50.3 us
    all_to_all x3, blocking collectives, spread(): lax.all_to_all(jnp.broadcast_to(x[None], (n, *x.shape)), axes, 0, 0, tile...  38.2 us
    ppermute x6, starting transfers between devices, partner(): return lax.ppermute(x, 'core', [(0, 1), (1, 0)])  21.5 us
    ppermute x6, starting transfers between devices, moved(): return lax.ppermute(x, ('zlo', 'zhi'), pairs)  21.1 us
    pallas_call x7, Pallas kernels, placed(): pl.pallas_call(functools.partial(place_kernel, counts, by, int(join)), ou...  7.37 us
    pallas_call x2, Pallas kernels, mixed(): pl.pallas_call(mix_kernel if extra else first_kernel, out_shape=(pltpu.VM...  3.4 us
  transfers between devices with their start and end apart: 12, of which 5 were waited for; matrix products, arithmetic and copies ran while one was open for 0% of the time, Pallas kernels for 4%

profile of v1, /device:TPU:1, one launch (start us, length us, event | category | flops | bytes accessed | tf_op | source)
XLA Modules:
  0.0 144.3 jit_solution(15532868722905214965)
XLA Ops:
  1.3 1.7 %mix.2.refs_0_ = bf16[1024,256]{1,0:T(8,128)(2,1)S(1)} custom-call(f32[1]{0:T(128)S(6)} %copy.34.share_ref, f32[256,1024]{1,0:T(8,128)} %bitcast.15, f32[256,1024]{1,0:T(8,128)} %bitcast.16), custom_call_target="tpu_custom_call" | custom-call | flops 1048576 | bytes 2621440 | tf_op jit(solution)/shard_map/mix/pallas_call | solution.py:59
  3.0 1.7 %mix.3 = (bf16[1024,256]{1,0:T(8,128)(2,1)S(1)}, bf16[2048,256]{1,0:T(8,128)(2,1)S(1)}) custom-call(f32[1]{0:T(128)S(6)} %copy.34.share_ref, f32[256,1024]{1,0:T(8,128)} %bitcast.17, f32[256,1024]{1,0:T(8,128)} %bitcast.18, bf16[1024,256]{1,0:T(8,128)(2,1)S(1)} %mix.2.refs_0_), custom_call_target="tpu_custom_call" | custom-call | flops 1048576 | bytes 2621440 | tf_op jit(solution)/shard_map/mix/pallas_call | solution.py:59
  4.7 8.7 %collective-permute-start.10 = (bf16[2048,256]{1,0:T(8,128)(2,1)S(1)}, bf16[2048,256]{1,0:T(8,128)(2,1)S(1)}, u32[]{:S(2)}, u32[]{:S(2)}) collective-permute-start(bf16[2048,256]{1,0:T(8,128)(2,1)S(1)} %get-tuple-element.21.refs_0_), channel_id=1, source_target_pairs={{0,1},{1,0},{2,3},{3,2},{4,5},{5,4},{6,7},{7,6},{8,9},{9,8},{10,11... | collective-permute-start | bytes 3145736 | tf_op jit(solution)/shard_map/ppermute | solution.py:175
  13.4 1.9 %collective-permute-start.2 = (bf16[1024,256]{1,0:T(8,128)(2,1)S(1)}, bf16[1024,256]{1,0:T(8,128)(2,1)S(1)}, u32[]{:S(2)}, u32[]{:S(2)}) collective-permute-start(bf16[1024,256]{1,0:T(8,128)(2,1)S(1)} %get-tuple-element.20), channel_id=1, source_target_pairs={{0,2},{2,4},{4,6},{6,0},{256,262},{258,256},{260,258},{262,260},{1... | collective-permute-start | bytes 1572872 | tf_op jit(solution)/shard_map/ppermute | solution.py:172
  15.4 5.6 %collective-permute-start.7 = (bf16[1024,256]{1,0:T(8,128)(2,1)S(1)}, bf16[1024,256]{1,0:T(8,128)(2,1)S(1)}, u32[]{:S(2)}, u32[]{:S(2)}) collective-permute-start(bf16[1024,256]{1,0:T(8,128)(2,1)S(1)} %mix.2.refs_0_), channel_id=1, source_target_pairs={{0,2},{2,4},{4,6},{6,0},{256,262},{258,256},{260,258},{262,260},{1... | collective-permute-start | bytes 1572872 | tf_op jit(solution)/shard_map/ppermute | solution.py:172
  20.9 1.0 place.7
  22.0 0.0 collective-permute-done.10.refs_0_
  22.0 1.0 place.8
  23.0 7.9 %collective-permute-done.2.refs_1_ = bf16[1024,256]{1,0:T(8,128)(2,1)S(1)} collective-permute-done((bf16[1024,256]{1,0:T(8,128)(2,1)S(1)}, bf16[1024,256]{1,0:T(8,128)(2,1)S(1)}, u32[]{:S(2)}, u32[]{:S(2)}) %collective-permute-start.2) | collective-permute-done | bytes 524320 | tf_op jit(solution)/shard_map/ppermute | solution.py:172
  30.9 11.2 %collective-permute-done.7.refs_0_ = bf16[1024,256]{1,0:T(8,128)(2,1)S(1)} collective-permute-done((bf16[1024,256]{1,0:T(8,128)(2,1)S(1)}, bf16[1024,256]{1,0:T(8,128)(2,1)S(1)}, u32[]{:S(2)}, u32[]{:S(2)}) %collective-permute-start.7) | collective-permute-done | bytes 524320 | tf_op jit(solution)/shard_map/ppermute | solution.py:172
  42.2 0.0 copy-start
  42.2 0.0 copy-start.1
  42.2 1.0 place.9
  43.2 2.8 %collective-permute-start.11 = (bf16[2048,256]{1,0:T(8,128)(2,1)S(1)}, bf16[2048,256]{1,0:T(8,128)(2,1)S(1)}, u32[]{:S(2)}, u32[]{:S(2)}) collective-permute-start(bf16[2048,256]{1,0:T(8,128)(2,1)S(1)} %get-tuple-element.26), channel_id=1, source_target_pairs={{0,1},{1,0},{2,3},{3,2},{4,5},{5,4},{6,7},{7,6},{8,9},{9,8},{10,11... | collective-permute-start | bytes 3145736 | tf_op jit(solution)/shard_map/ppermute | solution.py:175
  46.0 1.9 %collective-permute-start.8 = (bf16[1024,256]{1,0:T(8,128)(2,1)S(1)}, bf16[1024,256]{1,0:T(8,128)(2,1)S(1)}, u32[]{:S(2)}, u32[]{:S(2)}) collective-permute-start(bf16[1024,256]{1,0:T(8,128)(2,1)S(1)} %collective-permute-done.7.refs_0_), channel_id=1, source_target_pairs={{0,2},{2,4},{4,6},{6,0},{256,262},{258,256},{260,258},{262,260},{1... | collective-permute-start | bytes 1572872 | tf_op jit(solution)/shard_map/ppermute | solution.py:172
  47.9 5.5 %collective-permute-start.5 = (bf16[1024,256]{1,0:T(8,128)(2,1)S(1)}, bf16[1024,256]{1,0:T(8,128)(2,1)S(1)}, u32[]{:S(2)}, u32[]{:S(2)}) collective-permute-start(bf16[1024,256]{1,0:T(8,128)(2,1)S(1)} %mix.2.refs_0_), channel_id=1, source_target_pairs={{0,6},{2,0},{4,2},{6,4},{256,258},{258,260},{260,262},{262,256},{1... | collective-permute-start | bytes 1572872 | tf_op jit(solution)/shard_map/ppermute | solution.py:172
  53.4 2.9 %collective-permute-start = (bf16[1024,256]{1,0:T(8,128)(2,1)S(1)}, bf16[1024,256]{1,0:T(8,128)(2,1)S(1)}, u32[]{:S(2)}, u32[]{:S(2)}) collective-permute-start(bf16[1024,256]{1,0:T(8,128)(2,1)S(1)} %get-tuple-element.20), channel_id=1, source_target_pairs={{0,6},{2,0},{4,2},{6,4},{256,258},{258,260},{260,262},{262,256},{1... | collective-permute-start | bytes 1572872 | tf_op jit(solution)/shard_map/ppermute | solution.py:172
  56.3 3.3 %collective-permute-start.3 = (bf16[1024,256]{1,0:T(8,128)(2,1)S(1)}, bf16[1024,256]{1,0:T(8,128)(2,1)S(1)}, u32[]{:S(2)}, u32[]{:S(2)}) collective-permute-start(bf16[1024,256]{1,0:T(8,128)(2,1)S(1)} %collective-permute-done.2.refs_1_), channel_id=1, source_target_pairs={{0,2},{2,4},{4,6},{6,0},{256,262},{258,256},{260,258},{262,260},{1... | collective-permute-start | bytes 1572872 | tf_op jit(solution)/shard_map/ppermute | solution.py:172
  59.6 4.1 %collective-permute-done.8.refs_0_ = bf16[1024,256]{1,0:T(8,128)(2,1)S(1)} collective-permute-done((bf16[1024,256]{1,0:T(8,128)(2,1)S(1)}, bf16[1024,256]{1,0:T(8,128)(2,1)S(1)}, u32[]{:S(2)}, u32[]{:S(2)}) %collective-permute-start.8) | collective-permute-done | bytes 524320 | tf_op jit(solution)/shard_map/ppermute | solution.py:172
  63.6 3.3 %collective-permute-start.9 = (bf16[1024,256]{1,0:T(8,128)(2,1)S(1)}, bf16[1024,256]{1,0:T(8,128)(2,1)S(1)}, u32[]{:S(2)}, u32[]{:S(2)}) collective-permute-start(bf16[1024,256]{1,0:T(8,128)(2,1)S(1)} %collective-permute-done.8.refs_0_), channel_id=1, source_target_pairs={{0,1},{1,0},{2,3},{3,2},{4,5},{5,4},{6,7},{7,6},{8,9},{9,8},{10,11... | collective-permute-start | bytes 1572872 | tf_op jit(solution)/shard_map/ppermute | solution.py:175
  66.9 18.2 %collective-permute-done.5.refs_2_ = bf16[1024,256]{1,0:T(8,128)(2,1)S(1)} collective-permute-done((bf16[1024,256]{1,0:T(8,128)(2,1)S(1)}, bf16[1024,256]{1,0:T(8,128)(2,1)S(1)}, u32[]{:S(2)}, u32[]{:S(2)}) %collective-permute-start.5) | collective-permute-done | bytes 524320 | tf_op jit(solution)/shard_map/ppermute | solution.py:172
  85.1 2.4 %collective-permute-start.6 = (bf16[1024,256]{1,0:T(8,128)(2,1)S(1)}, bf16[1024,256]{1,0:T(8,128)(2,1)S(1)}, u32[]{:S(2)}, u32[]{:S(2)}) collective-permute-start(bf16[1024,256]{1,0:T(8,128)(2,1)S(1)} %collective-permute-done.5.refs_2_), channel_id=1, source_target_pairs={{0,1},{1,0},{2,3},{3,2},{4,5},{5,4},{6,7},{7,6},{8,9},{9,8},{10,11... | collective-permute-start | bytes 1572872 | tf_op jit(solution)/shard_map/ppermute | solution.py:175
  87.5 8.9 %collective-permute-done.refs_1_ = bf16[1024,256]{1,0:T(8,128)(2,1)S(1)} collective-permute-done((bf16[1024,256]{1,0:T(8,128)(2,1)S(1)}, bf16[1024,256]{1,0:T(8,128)(2,1)S(1)}, u32[]{:S(2)}, u32[]{:S(2)}) %collective-permute-start) | collective-permute-done | bytes 524320 | tf_op jit(solution)/shard_map/ppermute | solution.py:172
  96.4 2.3 %collective-permute-start.1 = (bf16[1024,256]{1,0:T(8,128)(2,1)S(1)}, bf16[1024,256]{1,0:T(8,128)(2,1)S(1)}, u32[]{:S(2)}, u32[]{:S(2)}) collective-permute-start(bf16[1024,256]{1,0:T(8,128)(2,1)S(1)} %collective-permute-done.refs_1_), channel_id=1, source_target_pairs={{0,1},{1,0},{2,3},{3,2},{4,5},{5,4},{6,7},{7,6},{8,9},{9,8},{10,11... | collective-permute-start | bytes 1572872 | tf_op jit(solution)/shard_map/ppermute | solution.py:175
  98.7 0.0 collective-permute-done.3.refs_2_
  98.7 2.0 %collective-permute-start.4 = (bf16[1024,256]{1,0:T(8,128)(2,1)S(1)}, bf16[1024,256]{1,0:T(8,128)(2,1)S(1)}, u32[]{:S(2)}, u32[]{:S(2)}) collective-permute-start(bf16[1024,256]{1,0:T(8,128)(2,1)S(1)} %collective-permute-done.3.refs_2_), channel_id=1, source_target_pairs={{0,1},{1,0},{2,3},{3,2},{4,5},{5,4},{6,7},{7,6},{8,9},{9,8},{10,11... | collective-permute-start | bytes 1572872 | tf_op jit(solution)/shard_map/ppermute | solution.py:175
  100.7 0.0 copy-done
  100.7 0.0 copy-done.1
  100.8 13.2 %all_to_all.15 = bf16[8,2,128]{2,1,0:T(2,128)(2,1)S(1)} all-to-all(bf16[8,2,128]{2,1,0:T(2,128)(2,1)S(1)} %broadcast_in_dim.34), channel_id=1, replica_groups=mesh['zlo'=2,'y'=8,'x'=4,'zhi'=4,'core'=2] {'y'}, dimensions={0} | all-to-all | bytes 8192 | tf_op jit(solution)/shard_map/all_to_all | solution.py:160
  114.0 15.0 %all_to_all.16 = bf16[16,16,128]{2,1,0:T(8,128)(2,1)S(1)} all-to-all(bf16[16,16,128]{2,1,0:T(8,128)(2,1)S(1)} %broadcast_in_dim.36), channel_id=1, replica_groups=mesh['zlo'=2,'y'=8,'x'=4,'zhi'=4,'core'=2] {'zlo','zhi','core'}, dimensions={0} | all-to-all | bytes 131072 | tf_op jit(solution)/shard_map/all_to_all | solution.py:160
  129.0 10.0 %all_to_all.17 = bf16[4,256,128]{2,1,0:T(8,128)(2,1)S(1)} all-to-all(bf16[4,256,128]{2,1,0:T(8,128)(2,1)S(1)} %broadcast_in_dim.38), channel_id=1, replica_groups=mesh['zlo'=2,'y'=8,'x'=4,'zhi'=4,'core'=2] {'x'}, dimensions={0} | all-to-all | bytes 524288 | tf_op jit(solution)/shard_map/all_to_all | solution.py:160
  139.0 0.8 order.1
  139.9 0.0 collective-permute-done.11.refs_0_
  139.9 1.0 place.10
  140.9 0.0 collective-permute-done.9.refs_1_
  140.9 1.2 place.11
  142.1 0.0 collective-permute-done.6.refs_0_
  142.1 1.2 place.12
  143.3 0.0 collective-permute-done.1.refs_0_
  143.3 0.0 collective-permute-done.4.refs_1_
  143.3 1.0 place.13
  (4 shorter events, 0.1 us)
Async XLA Ops:
  4.7 17.3 %collective-permute-start.10 = (bf16[2048,256]{1,0:T(8,128)(2,1)S(1)}, bf16[2048,256]{1,0:T(8,128)(2,1)S(1)}, u32[]{:S(2)}, u32[]{:S(2)}) collective-permute-start(bf16[2048,256]{1,0:T(8,128)(2,1)S(1)} %get-tuple-element.21.refs_0_), channel_id=1, source_target_pairs={{0,1},{1,0},{2,3},{3,2},{4,5},{5,4},{6,7},{7,6},{8,9},{9,8},{10,11... | collective-permute-start | bytes 3145736 | tf_op jit(solution)/shard_map/ppermute | solution.py:175
  13.4 17.5 %collective-permute-start.2 = (bf16[1024,256]{1,0:T(8,128)(2,1)S(1)}, bf16[1024,256]{1,0:T(8,128)(2,1)S(1)}, u32[]{:S(2)}, u32[]{:S(2)}) collective-permute-start(bf16[1024,256]{1,0:T(8,128)(2,1)S(1)} %get-tuple-element.20), channel_id=1, source_target_pairs={{0,2},{2,4},{4,6},{6,0},{256,262},{258,256},{260,258},{262,260},{1... | collective-permute-start | bytes 1572872 | tf_op jit(solution)/shard_map/ppermute | solution.py:172
  15.4 26.8 %collective-permute-start.7 = (bf16[1024,256]{1,0:T(8,128)(2,1)S(1)}, bf16[1024,256]{1,0:T(8,128)(2,1)S(1)}, u32[]{:S(2)}, u32[]{:S(2)}) collective-permute-start(bf16[1024,256]{1,0:T(8,128)(2,1)S(1)} %mix.2.refs_0_), channel_id=1, source_target_pairs={{0,2},{2,4},{4,6},{6,0},{256,262},{258,256},{260,258},{262,260},{1... | collective-permute-start | bytes 1572872 | tf_op jit(solution)/shard_map/ppermute | solution.py:172
  42.2 58.6 %copy-start = (f32[256,1]{0,1:T(1,128)S(1)}, f32[256,1]{0,1:T(1,128)}, u32[]{:S(2)}) copy-start(f32[256,1]{0,1:T(1,128)} %param.12) | copy-start | bytes 3076
  42.2 58.6 %copy-start.1 = (f32[256]{0:T(256)S(1)}, f32[256]{0:T(256)}, u32[]{:S(2)}) copy-start(f32[256]{0:T(256)} %param.13) | copy-start | bytes 3076
  43.2 96.7 %collective-permute-start.11 = (bf16[2048,256]{1,0:T(8,128)(2,1)S(1)}, bf16[2048,256]{1,0:T(8,128)(2,1)S(1)}, u32[]{:S(2)}, u32[]{:S(2)}) collective-permute-start(bf16[2048,256]{1,0:T(8,128)(2,1)S(1)} %get-tuple-element.26), channel_id=1, source_target_pairs={{0,1},{1,0},{2,3},{3,2},{4,5},{5,4},{6,7},{7,6},{8,9},{9,8},{10,11... | collective-permute-start | bytes 3145736 | tf_op jit(solution)/shard_map/ppermute | solution.py:175
  46.0 17.7 %collective-permute-start.8 = (bf16[1024,256]{1,0:T(8,128)(2,1)S(1)}, bf16[1024,256]{1,0:T(8,128)(2,1)S(1)}, u32[]{:S(2)}, u32[]{:S(2)}) collective-permute-start(bf16[1024,256]{1,0:T(8,128)(2,1)S(1)} %collective-permute-done.7.refs_0_), channel_id=1, source_target_pairs={{0,2},{2,4},{4,6},{6,0},{256,262},{258,256},{260,258},{262,260},{1... | collective-permute-start | bytes 1572872 | tf_op jit(solution)/shard_map/ppermute | solution.py:172
  47.9 37.2 %collective-permute-start.5 = (bf16[1024,256]{1,0:T(8,128)(2,1)S(1)}, bf16[1024,256]{1,0:T(8,128)(2,1)S(1)}, u32[]{:S(2)}, u32[]{:S(2)}) collective-permute-start(bf16[1024,256]{1,0:T(8,128)(2,1)S(1)} %mix.2.refs_0_), channel_id=1, source_target_pairs={{0,6},{2,0},{4,2},{6,4},{256,258},{258,260},{260,262},{262,256},{1... | collective-permute-start | bytes 1572872 | tf_op jit(solution)/shard_map/ppermute | solution.py:172
  53.4 43.0 %collective-permute-start = (bf16[1024,256]{1,0:T(8,128)(2,1)S(1)}, bf16[1024,256]{1,0:T(8,128)(2,1)S(1)}, u32[]{:S(2)}, u32[]{:S(2)}) collective-permute-start(bf16[1024,256]{1,0:T(8,128)(2,1)S(1)} %get-tuple-element.20), channel_id=1, source_target_pairs={{0,6},{2,0},{4,2},{6,4},{256,258},{258,260},{260,262},{262,256},{1... | collective-permute-start | bytes 1572872 | tf_op jit(solution)/shard_map/ppermute | solution.py:172
  56.3 42.4 %collective-permute-start.3 = (bf16[1024,256]{1,0:T(8,128)(2,1)S(1)}, bf16[1024,256]{1,0:T(8,128)(2,1)S(1)}, u32[]{:S(2)}, u32[]{:S(2)}) collective-permute-start(bf16[1024,256]{1,0:T(8,128)(2,1)S(1)} %collective-permute-done.2.refs_1_), channel_id=1, source_target_pairs={{0,2},{2,4},{4,6},{6,0},{256,262},{258,256},{260,258},{262,260},{1... | collective-permute-start | bytes 1572872 | tf_op jit(solution)/shard_map/ppermute | solution.py:172
  63.6 77.2 %collective-permute-start.9 = (bf16[1024,256]{1,0:T(8,128)(2,1)S(1)}, bf16[1024,256]{1,0:T(8,128)(2,1)S(1)}, u32[]{:S(2)}, u32[]{:S(2)}) collective-permute-start(bf16[1024,256]{1,0:T(8,128)(2,1)S(1)} %collective-permute-done.8.refs_0_), channel_id=1, source_target_pairs={{0,1},{1,0},{2,3},{3,2},{4,5},{5,4},{6,7},{7,6},{8,9},{9,8},{10,11... | collective-permute-start | bytes 1572872 | tf_op jit(solution)/shard_map/ppermute | solution.py:175
  85.1 56.9 %collective-permute-start.6 = (bf16[1024,256]{1,0:T(8,128)(2,1)S(1)}, bf16[1024,256]{1,0:T(8,128)(2,1)S(1)}, u32[]{:S(2)}, u32[]{:S(2)}) collective-permute-start(bf16[1024,256]{1,0:T(8,128)(2,1)S(1)} %collective-permute-done.5.refs_2_), channel_id=1, source_target_pairs={{0,1},{1,0},{2,3},{3,2},{4,5},{5,4},{6,7},{7,6},{8,9},{9,8},{10,11... | collective-permute-start | bytes 1572872 | tf_op jit(solution)/shard_map/ppermute | solution.py:175
  96.4 46.9 %collective-permute-start.1 = (bf16[1024,256]{1,0:T(8,128)(2,1)S(1)}, bf16[1024,256]{1,0:T(8,128)(2,1)S(1)}, u32[]{:S(2)}, u32[]{:S(2)}) collective-permute-start(bf16[1024,256]{1,0:T(8,128)(2,1)S(1)} %collective-permute-done.refs_1_), channel_id=1, source_target_pairs={{0,1},{1,0},{2,3},{3,2},{4,5},{5,4},{6,7},{7,6},{8,9},{9,8},{10,11... | collective-permute-start | bytes 1572872 | tf_op jit(solution)/shard_map/ppermute | solution.py:175
  98.7 44.6 %collective-permute-start.4 = (bf16[1024,256]{1,0:T(8,128)(2,1)S(1)}, bf16[1024,256]{1,0:T(8,128)(2,1)S(1)}, u32[]{:S(2)}, u32[]{:S(2)}) collective-permute-start(bf16[1024,256]{1,0:T(8,128)(2,1)S(1)} %collective-permute-done.3.refs_2_), channel_id=1, source_target_pairs={{0,1},{1,0},{2,3},{3,2},{4,5},{5,4},{6,7},{7,6},{8,9},{9,8},{10,11... | collective-permute-start | bytes 1572872 | tf_op jit(solution)/shard_map/ppermute | solution.py:175

commit v2 on v1

--- a/solution.py
+++ b/solution.py
@@ -18,6 +18,7 @@
 VMEM = pl.BlockSpec(memory_space=pltpu.VMEM)
 SMEM = pl.BlockSpec(memory_space=pltpu.SMEM)
 GATE, UP = 0, 1
+AHEAD = -1
 
 
 def mix_kernel(share_ref, w_ref, avg_ref, *refs):
@@ -72,12 +73,13 @@
 
 
 def place_kernel(counts, by, join, *refs):
-    outs, sems = refs[-3 - join : -1 - join], refs[-1]
+    extra = 1 if join else 0
+    outs, sems = refs[-3 - extra : -1 - extra], refs[-1]
     joined = refs[-2] if join else None
     width = refs[0].shape[1]
     chips = lax.axis_size("zhi")
     chip, core = lax.axis_index("zhi"), lax.axis_index("core")
-    sign = 1 - 2 * lax.axis_index("zlo")
+    sign = AHEAD * (1 - 2 * lax.axis_index("zlo"))
     copies, pieces, at = [], [], 0
     entries = iter(by)
     for ref, count in zip(refs, counts):
@@ -93,25 +95,26 @@
     for c in copies:
         c.start()
     if join:
-        for piece, size in pieces:
+        for piece, size in pieces[:join]:
             joined[pl.ds(at, size), :] = piece[...]
             at += size
     for c in copies:
         c.wait()
 
 
-def placed(outs, arrays, columns, rows, join=False):
+def placed(outs, arrays, columns, rows, join=0):
     n = len(arrays)
     by = tuple(p for _, pieces in arrays for p in pieces)
     counts = tuple(len(pieces) for _, pieces in arrays)
     arrays = [pltpu.with_memory_space_constraint(a, pltpu.VMEM) for a, _ in arrays]
     width = arrays[0].shape[1]
     total = sum(p[2] for p in by)
+    joined = sum(p[2] for p in by[:join])
     out = jax.ShapeDtypeStruct((rows, columns), BF16)
     extra = () if outs is None else tuple(outs)
     res = pl.pallas_call(
-        functools.partial(place_kernel, counts, by, int(join)),
-        out_shape=(out, out) + ((pltpu.VMEM((total, width), BF16),) if join else ()),
+        functools.partial(place_kernel, counts, by, join),
+        out_shape=(out, out) + ((pltpu.VMEM((joined, width), BF16),) if join else ()),
         in_specs=[VMEM] * n + [ANY] * len(extra),
         out_specs=(ANY, ANY) + ((VMEM,) if join else ()),
         input_output_aliases={n + i: i for i in range(len(extra))},
@@ -123,31 +126,26 @@
     return res[:2], (res[2] if join else None)
 
 
-def order_kernel(nx, ny, nz, in_ref, out_ref, wide, turned):
+def order_kernel(nxy, nz, in_ref, out_ref, wide):
     lanes = in_ref.shape[1]
     wide[...] = in_ref[...].astype(jnp.float32)
-    shards = in_ref.shape[0] // (nx * ny * nz * 2)
-    for x in range(nx):
-        for z in range(nz):
-            for s in range(shards):
-                for h in range(2):
-                    rows = wide[pl.ds(((x * nz + z) * shards + s) * ny * 2 + h, ny, stride=2), :]
-                    turned[s * 2 + h, pl.ds(z * ny * nx + x, ny, stride=nx), :] = rows
-    for j in range(2 * shards):
-        out_ref[:, pl.ds(j * lanes, lanes)] = turned[j].astype(BF16)
-
-
-def ordered(part, nx, ny, nz):
+    column = in_ref.shape[0] // nxy
+    for z in range(nz):
+        for j in range(column // nz):
+            rows = wide[pl.ds(z * (column // nz) + j, nxy, stride=column), :]
+            out_ref[pl.ds(z * nxy, nxy), pl.ds(j * lanes, lanes)] = rows.astype(BF16)
+
+
+def ordered(part, nxy, nz):
     rows, lanes = part.shape
-    experts = nx * ny * nz
+    experts = nxy * nz
     return pl.pallas_call(
-        functools.partial(order_kernel, nx, ny, nz),
+        functools.partial(order_kernel, nxy, nz),
         out_shape=jax.ShapeDtypeStruct((experts, rows * lanes // experts), BF16),
         in_specs=[VMEM],
         out_specs=VMEM,
         scratch_shapes=[
             pltpu.VMEM((rows, lanes), jnp.float32),
-            pltpu.VMEM((rows // experts, experts, lanes), jnp.float32),
         ],
         compiler_params=pltpu.CompilerParams(vmem_limit_bytes=4 << 20),
         cost_estimate=pl.CostEstimate(flops=rows * lanes, bytes_accessed=4 * rows * lanes, transcendentals=0),
@@ -174,7 +172,7 @@
     def partner(x):
         return lax.ppermute(x, "core", [(0, 1), (1, 0)])
 
-    def place(outs, *arrays, join=False):
+    def place(outs, *arrays, join=0):
         return placed(outs, arrays, columns, rows, join)
 
     def pieces(step, other, *which):
@@ -182,32 +180,30 @@
 
     (gate,) = mixed(mix_share, w_gate[0], avg_gate[0])
     up, own = mixed(mix_share, w_up[0], avg_up[0], gate)
-    a1 = moved(gate, 1)
-    a2 = moved(up, 1)
-    c1 = moved(a1, 1)
-    c2 = moved(a2, 1)
-    b1 = moved(gate, -1)
-    b2 = moved(up, -1)
+    a1 = moved(gate, AHEAD)
+    a2 = moved(up, AHEAD)
+    c1 = moved(a1, AHEAD)
+    c2 = moved(a2, AHEAD)
+    f1 = moved(c1, AHEAD)
+    f2 = moved(c2, AHEAD)
 
     nx, ny, nz = (lax.axis_size(a) for a in ("x", "y", "zlo"))
     part = (router_weight * router_gain[:, None]).astype(BF16).reshape(2, -1)
     lanes = part.shape[1]
-    part = spread(part, ("y",)).reshape(-1, lanes)
     part = spread(part, ("zlo", "zhi", "core")).reshape(-1, lanes)
-    part = spread(part, ("x",)).reshape(-1, lanes)
-    serve_router = ordered(part, nx, ny, nz).T
+    part = spread(part, ("y", "x")).reshape(-1, lanes)
+    serve_router = ordered(part, nx * ny, nz).T
 
     outs, _ = place(None, (own, pieces(0, 0, GATE, UP)))
-    outs, _ = place(outs, (partner(own), pieces(0, 1, GATE, UP)))
-    outs, both = place(outs, (a1, pieces(1, 0, GATE)), (a2, pieces(1, 0, UP)), join=True)
+    outs, both = place(
+        outs, (a1, pieces(1, 0, GATE)), (a2, pieces(1, 0, UP)), (partner(own), pieces(0, 1, GATE, UP)), join=2
+    )
     outs, _ = place(outs, (partner(both), pieces(1, 1, GATE, UP)))
-    c1_other = partner(c1)
-    b1_other = partner(b1)
-    b2_other = partner(b2)
-    c2_other = partner(c2)
-    outs, _ = place(outs, (c1, pieces(2, 0, GATE)), (c1_other, pieces(2, 1, GATE)), (b1, pieces(-1, 0, GATE)))
-    outs, _ = place(outs, (b1_other, pieces(-1, 1, GATE)), (b2, pieces(-1, 0, UP)), (c2, pieces(2, 0, UP)))
-    outs, _ = place(outs, (b2_other, pieces(-1, 1, UP)), (c2_other, pieces(2, 1, UP)))
+    outs, both = place(outs, (c1, pieces(2, 0, GATE)), (c2, pieces(2, 0, UP)), join=2)
+    both_other, f1_other, f2_other = partner(both), partner(f1), partner(f2)
+    outs, _ = place(outs, (both_other, pieces(2, 1, GATE, UP)), (f1, pieces(3, 0, GATE)))
+    outs, _ = place(outs, (f1_other, pieces(3, 1, GATE)), (f2, pieces(3, 0, UP)))
+    outs, _ = place(outs, (f2_other, pieces(3, 1, UP)))
     return outs[0][None], outs[1][None], serve_router
 
 

time: 145 us -> 138 us (0.952)
  waiting for transfers between devices: 50.3 us -> 41.6 us
  starting transfers between devices: 42.5 us -> 48.5 us
  blocking collectives: 38.2 us -> 33.6 us
    ppermute x6, waiting for transfers between devices: 50.3 us -> 41.6 us  [moved(): return lax.ppermute(x, ('zlo', 'zhi'), pairs)]
    ppermute x6, starting transfers between devices: 21.1 us -> 28 us  [moved(): return lax.ppermute(x, ('zlo', 'zhi'), pairs)]
    all_to_all x3 -> x2, blocking collectives: 38.2 us -> 33.6 us  [spread(): lax.all_to_all(jnp.broadcast_to(x[None], (n, *x.shape)), axes, 0, 0, tile...]
    ppermute x6 -> x5, starting transfers between devices: 21.5 us -> 20.5 us  [partner(): return lax.ppermute(x, 'core', [(0, 1), (1, 0)])]
  transfers between devices with their start and end apart: 12 -> 11, of which waited for: 5 -> 5; matrix products, arithmetic and copies ran while one was open for 0% -> 0% of each run, Pallas kernels for 4% -> 5%
where the time goes in v2:
time: 138 us; the launch traced here: 137 us
  starting transfers between devices  48.5 us (35%)
  waiting for transfers between devices  41.6 us (30%)
  blocking collectives  33.6 us (24%)
  Pallas kernels  11.8 us (9%)
  between operations  1.5 us (1%)
    ppermute x6, waiting for transfers between devices, moved(): return lax.ppermute(x, ('zlo', 'zhi'), pairs)  41.6 us
    all_to_all x2, blocking collectives, spread(): lax.all_to_all(jnp.broadcast_to(x[None], (n, *x.shape)), axes, 0, 0, tile...  33.6 us
    ppermute x6, starting transfers between devices, moved(): return lax.ppermute(x, ('zlo', 'zhi'), pairs)  28 us
    ppermute x5, starting transfers between devices, partner(): return lax.ppermute(x, 'core', [(0, 1), (1, 0)])  20.5 us
    pallas_call x7, Pallas kernels, placed(): pl.pallas_call(functools.partial(place_kernel, counts, by, join), out_sha...  7.39 us
    pallas_call x2, Pallas kernels, mixed(): pl.pallas_call(mix_kernel if extra else first_kernel, out_shape=(pltpu.VM...  3.4 us
  transfers between devices with their start and end apart: 11, of which 5 were waited for; matrix products, arithmetic and copies ran while one was open for 0% of the time, Pallas kernels for 5%

profile of v2, /device:TPU:1, one launch (start us, length us, event | category | flops | bytes accessed | tf_op | source)
XLA Modules:
  0.0 137.2 jit_solution(8713677937538157605)
XLA Ops:
  1.3 1.7 %mix.2.refs_0_ = bf16[1024,256]{1,0:T(8,128)(2,1)S(1)} custom-call(f32[1]{0:T(128)S(6)} %copy.34.share_ref, f32[256,1024]{1,0:T(8,128)} %bitcast.14, f32[256,1024]{1,0:T(8,128)} %bitcast.15), custom_call_target="tpu_custom_call" | custom-call | flops 1048576 | bytes 2621440 | tf_op jit(solution)/shard_map/mix/pallas_call | solution.py:60
  3.0 1.7 %mix.3 = (bf16[1024,256]{1,0:T(8,128)(2,1)S(1)}, bf16[2048,256]{1,0:T(8,128)(2,1)S(1)}) custom-call(f32[1]{0:T(128)S(6)} %copy.34.share_ref, f32[256,1024]{1,0:T(8,128)} %bitcast.16, f32[256,1024]{1,0:T(8,128)} %bitcast.17, bf16[1024,256]{1,0:T(8,128)(2,1)S(1)} %mix.2.refs_0_), custom_call_target="tpu_custom_call" | custom-call | flops 1048576 | bytes 2621440 | tf_op jit(solution)/shard_map/mix/pallas_call | solution.py:60
  4.7 8.7 %collective-permute-start.8 = (bf16[2048,256]{1,0:T(8,128)(2,1)S(1)}, bf16[2048,256]{1,0:T(8,128)(2,1)S(1)}, u32[]{:S(2)}, u32[]{:S(2)}) collective-permute-start(bf16[2048,256]{1,0:T(8,128)(2,1)S(1)} %get-tuple-element.22.refs_0_), channel_id=1, source_target_pairs={{0,1},{1,0},{2,3},{3,2},{4,5},{5,4},{6,7},{7,6},{8,9},{9,8},{10,11... | collective-permute-start | bytes 3145736 | tf_op jit(solution)/shard_map/ppermute | solution.py:173
  13.4 5.3 %collective-permute-start = (bf16[1024,256]{1,0:T(8,128)(2,1)S(1)}, bf16[1024,256]{1,0:T(8,128)(2,1)S(1)}, u32[]{:S(2)}, u32[]{:S(2)}) collective-permute-start(bf16[1024,256]{1,0:T(8,128)(2,1)S(1)} %get-tuple-element.21), channel_id=1, source_target_pairs={{0,6},{2,0},{4,2},{6,4},{256,258},{258,260},{260,262},{262,256},{1... | collective-permute-start | bytes 1572872 | tf_op jit(solution)/shard_map/ppermute | solution.py:170
  18.8 2.2 %collective-permute-start.4 = (bf16[1024,256]{1,0:T(8,128)(2,1)S(1)}, bf16[1024,256]{1,0:T(8,128)(2,1)S(1)}, u32[]{:S(2)}, u32[]{:S(2)}) collective-permute-start(bf16[1024,256]{1,0:T(8,128)(2,1)S(1)} %mix.2.refs_0_), channel_id=1, source_target_pairs={{0,6},{2,0},{4,2},{6,4},{256,258},{258,260},{260,262},{262,256},{1... | collective-permute-start | bytes 1572872 | tf_op jit(solution)/shard_map/ppermute | solution.py:170
  20.9 1.0 place.7
  22.0 8.1 %collective-permute-done.refs_1_ = bf16[1024,256]{1,0:T(8,128)(2,1)S(1)} collective-permute-done((bf16[1024,256]{1,0:T(8,128)(2,1)S(1)}, bf16[1024,256]{1,0:T(8,128)(2,1)S(1)}, u32[]{:S(2)}, u32[]{:S(2)}) %collective-permute-start) | collective-permute-done | bytes 524320 | tf_op jit(solution)/shard_map/ppermute | solution.py:170
  30.0 11.2 %collective-permute-done.4.refs_0_ = bf16[1024,256]{1,0:T(8,128)(2,1)S(1)} collective-permute-done((bf16[1024,256]{1,0:T(8,128)(2,1)S(1)}, bf16[1024,256]{1,0:T(8,128)(2,1)S(1)}, u32[]{:S(2)}, u32[]{:S(2)}) %collective-permute-start.4) | collective-permute-done | bytes 524320 | tf_op jit(solution)/shard_map/ppermute | solution.py:170
  41.2 0.0 collective-permute-done.8.refs_2_
  41.3 1.4 %place.8 = (bf16[1024,2048]{1,0:T(8,128)(2,1)}, bf16[1024,2048]{1,0:T(8,128)(2,1)}, bf16[2048,256]{1,0:T(8,128)(2,1)S(1)}) custom-call(bf16[1024,256]{1,0:T(8,128)(2,1)S(1)} %collective-permute-done.4.refs_0_, bf16[1024,256]{1,0:T(8,128)(2,1)S(1)} %collective-permute-done.refs_1_, ...), custom_call_target="tpu_custom_call", output_to_operand_aliasing={{0}: (3, {}), {1}: (4, {})} | custom-call | flops 2097152 | bytes 4194304 | tf_op jit(solution)/shard_map/place/pallas_call | solution.py:115
  42.6 2.8 %collective-permute-start.9 = (bf16[2048,256]{1,0:T(8,128)(2,1)S(1)}, bf16[2048,256]{1,0:T(8,128)(2,1)S(1)}, u32[]{:S(2)}, u32[]{:S(2)}) collective-permute-start(bf16[2048,256]{1,0:T(8,128)(2,1)S(1)} %get-tuple-element.25), channel_id=1, source_target_pairs={{0,1},{1,0},{2,3},{3,2},{4,5},{5,4},{6,7},{7,6},{8,9},{9,8},{10,11... | collective-permute-start | bytes 3145736 | tf_op jit(solution)/shard_map/ppermute | solution.py:173
  45.4 6.2 %collective-permute-start.5 = (bf16[1024,256]{1,0:T(8,128)(2,1)S(1)}, bf16[1024,256]{1,0:T(8,128)(2,1)S(1)}, u32[]{:S(2)}, u32[]{:S(2)}) collective-permute-start(bf16[1024,256]{1,0:T(8,128)(2,1)S(1)} %collective-permute-done.4.refs_0_), channel_id=1, source_target_pairs={{0,6},{2,0},{4,2},{6,4},{256,258},{258,260},{260,262},{262,256},{1... | collective-permute-start | bytes 1572872 | tf_op jit(solution)/shard_map/ppermute | solution.py:170
  51.7 1.9 %collective-permute-start.1 = (bf16[1024,256]{1,0:T(8,128)(2,1)S(1)}, bf16[1024,256]{1,0:T(8,128)(2,1)S(1)}, u32[]{:S(2)}, u32[]{:S(2)}) collective-permute-start(bf16[1024,256]{1,0:T(8,128)(2,1)S(1)} %collective-permute-done.refs_1_), channel_id=1, source_target_pairs={{0,6},{2,0},{4,2},{6,4},{256,258},{258,260},{260,262},{262,256},{1... | collective-permute-start | bytes 1572872 | tf_op jit(solution)/shard_map/ppermute | solution.py:170
  53.6 9.3 %collective-permute-done.5.refs_0_ = bf16[1024,256]{1,0:T(8,128)(2,1)S(1)} collective-permute-done((bf16[1024,256]{1,0:T(8,128)(2,1)S(1)}, bf16[1024,256]{1,0:T(8,128)(2,1)S(1)}, u32[]{:S(2)}, u32[]{:S(2)}) %collective-permute-start.5) | collective-permute-done | bytes 524320 | tf_op jit(solution)/shard_map/ppermute | solution.py:170
  62.9 6.2 %collective-permute-start.6 = (bf16[1024,256]{1,0:T(8,128)(2,1)S(1)}, bf16[1024,256]{1,0:T(8,128)(2,1)S(1)}, u32[]{:S(2)}, u32[]{:S(2)}) collective-permute-start(bf16[1024,256]{1,0:T(8,128)(2,1)S(1)} %collective-permute-done.5.refs_0_), channel_id=1, source_target_pairs={{0,6},{2,0},{4,2},{6,4},{256,258},{258,260},{260,262},{262,256},{1... | collective-permute-start | bytes 1572872 | tf_op jit(solution)/shard_map/ppermute | solution.py:170
  69.1 5.0 %collective-permute-done.1.refs_1_ = bf16[1024,256]{1,0:T(8,128)(2,1)S(1)} collective-permute-done((bf16[1024,256]{1,0:T(8,128)(2,1)S(1)}, bf16[1024,256]{1,0:T(8,128)(2,1)S(1)}, u32[]{:S(2)}, u32[]{:S(2)}) %collective-permute-start.1) | collective-permute-done | bytes 524320 | tf_op jit(solution)/shard_map/ppermute | solution.py:170
  74.1 6.2 %collective-permute-start.2 = (bf16[1024,256]{1,0:T(8,128)(2,1)S(1)}, bf16[1024,256]{1,0:T(8,128)(2,1)S(1)}, u32[]{:S(2)}, u32[]{:S(2)}) collective-permute-start(bf16[1024,256]{1,0:T(8,128)(2,1)S(1)} %collective-permute-done.1.refs_1_), channel_id=1, source_target_pairs={{0,6},{2,0},{4,2},{6,4},{256,258},{258,260},{260,262},{262,256},{1... | collective-permute-start | bytes 1572872 | tf_op jit(solution)/shard_map/ppermute | solution.py:170
  80.3 0.0 collective-permute-done.9.refs_0_
  80.4 1.0 place.9
  81.4 0.0 copy-start
  81.4 0.0 copy-start.1
  81.4 1.0 place.10
  82.4 3.5 %collective-permute-start.10 = (bf16[2048,256]{1,0:T(8,128)(2,1)S(1)}, bf16[2048,256]{1,0:T(8,128)(2,1)S(1)}, u32[]{:S(2)}, u32[]{:S(2)}) collective-permute-start(bf16[2048,256]{1,0:T(8,128)(2,1)S(1)} %get-tuple-element.30), channel_id=1, source_target_pairs={{0,1},{1,0},{2,3},{3,2},{4,5},{5,4},{6,7},{7,6},{8,9},{9,8},{10,11... | collective-permute-start | bytes 3145736 | tf_op jit(solution)/shard_map/ppermute | solution.py:173
  86.0 0.0 collective-permute-done.6.refs_1_
  86.0 2.6 %collective-permute-start.7 = (bf16[1024,256]{1,0:T(8,128)(2,1)S(1)}, bf16[1024,256]{1,0:T(8,128)(2,1)S(1)}, u32[]{:S(2)}, u32[]{:S(2)}) collective-permute-start(bf16[1024,256]{1,0:T(8,128)(2,1)S(1)} %collective-permute-done.6.refs_1_), channel_id=1, source_target_pairs={{0,1},{1,0},{2,3},{3,2},{4,5},{5,4},{6,7},{7,6},{8,9},{9,8},{10,11... | collective-permute-start | bytes 1572872 | tf_op jit(solution)/shard_map/ppermute | solution.py:173
  88.6 8.0 %collective-permute-done.2.refs_1_ = bf16[1024,256]{1,0:T(8,128)(2,1)S(1)} collective-permute-done((bf16[1024,256]{1,0:T(8,128)(2,1)S(1)}, bf16[1024,256]{1,0:T(8,128)(2,1)S(1)}, u32[]{:S(2)}, u32[]{:S(2)}) %collective-permute-start.2) | collective-permute-done | bytes 524320 | tf_op jit(solution)/shard_map/ppermute | solution.py:170
  96.6 2.8 %collective-permute-start.3 = (bf16[1024,256]{1,0:T(8,128)(2,1)S(1)}, bf16[1024,256]{1,0:T(8,128)(2,1)S(1)}, u32[]{:S(2)}, u32[]{:S(2)}) collective-permute-start(bf16[1024,256]{1,0:T(8,128)(2,1)S(1)} %collective-permute-done.2.refs_1_), channel_id=1, source_target_pairs={{0,1},{1,0},{2,3},{3,2},{4,5},{5,4},{6,7},{7,6},{8,9},{9,8},{10,11... | collective-permute-start | bytes 1572872 | tf_op jit(solution)/shard_map/ppermute | solution.py:173
  99.4 0.0 copy-done
  99.4 0.0 copy-done.1
  99.4 12.8 %all_to_all.10 = bf16[16,2,128]{2,1,0:T(2,128)(2,1)S(1)} all-to-all(bf16[16,2,128]{2,1,0:T(2,128)(2,1)S(1)} %broadcast_in_dim.27), channel_id=1, replica_groups=mesh['zlo'=2,'y'=8,'x'=4,'zhi'=4,'core'=2] {'zlo','zhi','core'}, dimensions={0} | all-to-all | bytes 16384 | tf_op jit(solution)/shard_map/all_to_all | solution.py:158
  112.3 20.8 %all_to_all.11 = bf16[32,32,128]{2,1,0:T(8,128)(2,1)S(1)} all-to-all(bf16[32,32,128]{2,1,0:T(8,128)(2,1)S(1)} %broadcast_in_dim.29), channel_id=1, replica_groups=mesh['zlo'=2,'y'=8,'x'=4,'zhi'=4,'core'=2] {'y','x'}, dimensions={0} | all-to-all | bytes 524288 | tf_op jit(solution)/shard_map/all_to_all | solution.py:158
  133.1 1.0 order.1
  134.1 0.0 collective-permute-done.10.refs_0_
  134.1 1.2 place.11
  135.3 0.0 collective-permute-done.7.refs_0_
  135.3 1.0 place.12
  136.3 0.0 collective-permute-done.3.refs_0_
  136.3 0.8 place.13
  (3 shorter events, 0.1 us)
Async XLA Ops:
  4.7 36.6 %collective-permute-start.8 = (bf16[2048,256]{1,0:T(8,128)(2,1)S(1)}, bf16[2048,256]{1,0:T(8,128)(2,1)S(1)}, u32[]{:S(2)}, u32[]{:S(2)}) collective-permute-start(bf16[2048,256]{1,0:T(8,128)(2,1)S(1)} %get-tuple-element.22.refs_0_), channel_id=1, source_target_pairs={{0,1},{1,0},{2,3},{3,2},{4,5},{5,4},{6,7},{7,6},{8,9},{9,8},{10,11... | collective-permute-start | bytes 3145736 | tf_op jit(solution)/shard_map/ppermute | solution.py:173
  13.4 16.6 %collective-permute-start = (bf16[1024,256]{1,0:T(8,128)(2,1)S(1)}, bf16[1024,256]{1,0:T(8,128)(2,1)S(1)}, u32[]{:S(2)}, u32[]{:S(2)}) collective-permute-start(bf16[1024,256]{1,0:T(8,128)(2,1)S(1)} %get-tuple-element.21), channel_id=1, source_target_pairs={{0,6},{2,0},{4,2},{6,4},{256,258},{258,260},{260,262},{262,256},{1... | collective-permute-start | bytes 1572872 | tf_op jit(solution)/shard_map/ppermute | solution.py:170
  18.8 22.5 %collective-permute-start.4 = (bf16[1024,256]{1,0:T(8,128)(2,1)S(1)}, bf16[1024,256]{1,0:T(8,128)(2,1)S(1)}, u32[]{:S(2)}, u32[]{:S(2)}) collective-permute-start(bf16[1024,256]{1,0:T(8,128)(2,1)S(1)} %mix.2.refs_0_), channel_id=1, source_target_pairs={{0,6},{2,0},{4,2},{6,4},{256,258},{258,260},{260,262},{262,256},{1... | collective-permute-start | bytes 1572872 | tf_op jit(solution)/shard_map/ppermute | solution.py:170
  42.6 37.7 %collective-permute-start.9 = (bf16[2048,256]{1,0:T(8,128)(2,1)S(1)}, bf16[2048,256]{1,0:T(8,128)(2,1)S(1)}, u32[]{:S(2)}, u32[]{:S(2)}) collective-permute-start(bf16[2048,256]{1,0:T(8,128)(2,1)S(1)} %get-tuple-element.25), channel_id=1, source_target_pairs={{0,1},{1,0},{2,3},{3,2},{4,5},{5,4},{6,7},{7,6},{8,9},{9,8},{10,11... | collective-permute-start | bytes 3145736 | tf_op jit(solution)/shard_map/ppermute | solution.py:173
  45.4 17.5 %collective-permute-start.5 = (bf16[1024,256]{1,0:T(8,128)(2,1)S(1)}, bf16[1024,256]{1,0:T(8,128)(2,1)S(1)}, u32[]{:S(2)}, u32[]{:S(2)}) collective-permute-start(bf16[1024,256]{1,0:T(8,128)(2,1)S(1)} %collective-permute-done.4.refs_0_), channel_id=1, source_target_pairs={{0,6},{2,0},{4,2},{6,4},{256,258},{258,260},{260,262},{262,256},{1... | collective-permute-start | bytes 1572872 | tf_op jit(solution)/shard_map/ppermute | solution.py:170
  51.7 22.5 %collective-permute-start.1 = (bf16[1024,256]{1,0:T(8,128)(2,1)S(1)}, bf16[1024,256]{1,0:T(8,128)(2,1)S(1)}, u32[]{:S(2)}, u32[]{:S(2)}) collective-permute-start(bf16[1024,256]{1,0:T(8,128)(2,1)S(1)} %collective-permute-done.refs_1_), channel_id=1, source_target_pairs={{0,6},{2,0},{4,2},{6,4},{256,258},{258,260},{260,262},{262,256},{1... | collective-permute-start | bytes 1572872 | tf_op jit(solution)/shard_map/ppermute | solution.py:170
  62.9 23.1 %collective-permute-start.6 = (bf16[1024,256]{1,0:T(8,128)(2,1)S(1)}, bf16[1024,256]{1,0:T(8,128)(2,1)S(1)}, u32[]{:S(2)}, u32[]{:S(2)}) collective-permute-start(bf16[1024,256]{1,0:T(8,128)(2,1)S(1)} %collective-permute-done.5.refs_0_), channel_id=1, source_target_pairs={{0,6},{2,0},{4,2},{6,4},{256,258},{258,260},{260,262},{262,256},{1... | collective-permute-start | bytes 1572872 | tf_op jit(solution)/shard_map/ppermute | solution.py:170
  74.1 22.5 %collective-permute-start.2 = (bf16[1024,256]{1,0:T(8,128)(2,1)S(1)}, bf16[1024,256]{1,0:T(8,128)(2,1)S(1)}, u32[]{:S(2)}, u32[]{:S(2)}) collective-permute-start(bf16[1024,256]{1,0:T(8,128)(2,1)S(1)} %collective-permute-done.1.refs_1_), channel_id=1, source_target_pairs={{0,6},{2,0},{4,2},{6,4},{256,258},{258,260},{260,262},{262,256},{1... | collective-permute-start | bytes 1572872 | tf_op jit(solution)/shard_map/ppermute | solution.py:170
  81.4 18.0 %copy-start = (f32[256,1]{0,1:T(1,128)S(1)}, f32[256,1]{0,1:T(1,128)}, u32[]{:S(2)}) copy-start(f32[256,1]{0,1:T(1,128)} %param.12) | copy-start | bytes 3076
  81.4 18.0 %copy-start.1 = (f32[256]{0:T(256)S(1)}, f32[256]{0:T(256)}, u32[]{:S(2)}) copy-start(f32[256]{0:T(256)} %param.13) | copy-start | bytes 3076
  82.4 51.7 %collective-permute-start.10 = (bf16[2048,256]{1,0:T(8,128)(2,1)S(1)}, bf16[2048,256]{1,0:T(8,128)(2,1)S(1)}, u32[]{:S(2)}, u32[]{:S(2)}) collective-permute-start(bf16[2048,256]{1,0:T(8,128)(2,1)S(1)} %get-tuple-element.30), channel_id=1, source_target_pairs={{0,1},{1,0},{2,3},{3,2},{4,5},{5,4},{6,7},{7,6},{8,9},{9,8},{10,11... | collective-permute-start | bytes 3145736 | tf_op jit(solution)/shard_map/ppermute | solution.py:173
  86.0 49.3 %collective-permute-start.7 = (bf16[1024,256]{1,0:T(8,128)(2,1)S(1)}, bf16[1024,256]{1,0:T(8,128)(2,1)S(1)}, u32[]{:S(2)}, u32[]{:S(2)}) collective-permute-start(bf16[1024,256]{1,0:T(8,128)(2,1)S(1)} %collective-permute-done.6.refs_1_), channel_id=1, source_target_pairs={{0,1},{1,0},{2,3},{3,2},{4,5},{5,4},{6,7},{7,6},{8,9},{9,8},{10,11... | collective-permute-start | bytes 1572872 | tf_op jit(solution)/shard_map/ppermute | solution.py:173
  96.6 39.7 %collective-permute-start.3 = (bf16[1024,256]{1,0:T(8,128)(2,1)S(1)}, bf16[1024,256]{1,0:T(8,128)(2,1)S(1)}, u32[]{:S(2)}, u32[]{:S(2)}) collective-permute-start(bf16[1024,256]{1,0:T(8,128)(2,1)S(1)} %collective-permute-done.2.refs_1_), channel_id=1, source_target_pairs={{0,1},{1,0},{2,3},{3,2},{4,5},{5,4},{6,7},{7,6},{8,9},{9,8},{10,11... | collective-permute-start | bytes 1572872 | tf_op jit(solution)/shard_map/ppermute | solution.py:173

commit v3 on v2

--- a/solution.py
+++ b/solution.py
@@ -10,7 +10,9 @@
 
 
 BF16 = jnp.bfloat16
-PIECES = 4
+WIDTH = 256
+HEAD = 256
+FIRST = 512
 EXPERT = ("zlo", "y", "x")
 SHARD = ("zhi", "core")
 ANY = pl.BlockSpec(memory_space=pl.ANY)
@@ -21,55 +23,85 @@
 AHEAD = -1
 
 
-def mix_kernel(share_ref, w_ref, avg_ref, *refs):
-    before, outs, (buf, sems) = refs[:-4], refs[-4:-2], refs[-2:]
-    rows = w_ref.shape[1]
-    width = rows // PIECES
-
-    def copies(piece):
-        cols = pl.ds(piece * width, width)
+def mix_kernel(plan, share_ref, *refs):
+    n = len(plan)
+    sources, before, outs, (buf, sems) = refs[: 2 * n], refs[2 * n : -4], refs[-4:-2], refs[-2:]
+    width = buf.shape[-1]
+    chunks, row = [], 0
+    for i, (first, size) in enumerate(plan):
+        for col in range(first, first + size, width):
+            chunks.append((sources[2 * i], sources[2 * i + 1], col, min(width, first + size - col), row))
+            row += chunks[-1][3]
+
+    def copies(k):
+        w, avg, col, size, _ = chunks[k]
         return [
-            pltpu.make_async_copy(src.at[:, cols], buf.at[i, piece], sems.at[i, piece])
-            for i, src in enumerate((w_ref, avg_ref))
+            pltpu.make_async_copy(src.at[:, pl.ds(col, size)], buf.at[i, k, :, pl.ds(0, size)], sems.at[i, k])
+            for i, src in enumerate((w, avg))
         ]
 
-    for piece in range(PIECES):
-        for c in copies(piece):
+    for k in range(len(chunks)):
+        for c in copies(k):
             c.start()
     share = share_ref[0]
     rest = 1.0 - share
-    for piece in range(PIECES):
-        for c in copies(piece):
+    for k, (_, _, _, size, at) in enumerate(chunks):
+        for c in copies(k):
             c.wait()
-        fresh = share * buf[0, piece] + rest * buf[1, piece]
-        turned = fresh.T.astype(BF16)
-        outs[0][pl.ds(piece * width, width), :] = turned
+        fresh = share * buf[0, k, :, :size] + rest * buf[1, k, :, :size]
+        turned = fresh.astype(BF16).T
+        outs[0][pl.ds(at, size), :] = turned
         if before:
-            outs[1][pl.ds(piece * width, width), :] = before[0][pl.ds(piece * width, width), :]
-            outs[1][pl.ds(rows + piece * width, width), :] = turned
-
-
-def first_kernel(share_ref, w_ref, avg_ref, out_ref, buf, sems):
-    mix_kernel(share_ref, w_ref, avg_ref, out_ref, None, buf, sems)
-
-
-def mixed(share, w, avg, before=None):
-    rows, cols = w.shape
-    w, avg = (pltpu.with_memory_space_constraint(x, pltpu.HBM) for x in (w, avg))
+            outs[1][pl.ds(before[0].shape[0] + at, size), :] = turned
+    if before:
+        outs[1][pl.ds(0, before[0].shape[0]), :] = before[0][...]
+
+
+def first_kernel(plan, *refs):
+    mix_kernel(plan, *refs[:-2], None, *refs[-2:])
+
+
+def mixed(share, sources, before=None):
+    rows = sources[0][0].shape[0]
+    plan = tuple((first, size) for _, _, first, size in sources)
+    total = sum(size for _, size in plan)
+    arrays = [pltpu.with_memory_space_constraint(x, pltpu.HBM) for w, avg, _, _ in sources for x in (w, avg)]
     extra = () if before is None else (pltpu.with_memory_space_constraint(before, pltpu.VMEM),)
+    chunks = sum(-(-size // WIDTH) for _, size in plan)
     return pl.pallas_call(
-        mix_kernel if extra else first_kernel,
-        out_shape=(pltpu.VMEM((cols, rows), BF16),) + ((pltpu.VMEM((2 * cols, rows), BF16),) if extra else ()),
-        in_specs=[SMEM, HBM, HBM] + [VMEM] * len(extra),
+        functools.partial(mix_kernel if extra else first_kernel, plan),
+        out_shape=(pltpu.VMEM((total, rows), BF16),)
+        + ((pltpu.VMEM((before.shape[0] + total, rows), BF16),) if extra else ()),
+        in_specs=[SMEM] + [HBM] * len(arrays) + [VMEM] * len(extra),
         out_specs=(VMEM,) * (1 + len(extra)),
         scratch_shapes=[
-            pltpu.VMEM((2, PIECES, rows, cols // PIECES), jnp.float32),
-            pltpu.SemaphoreType.DMA((2, PIECES)),
+            pltpu.VMEM((2, chunks, rows, WIDTH), jnp.float32),
+            pltpu.SemaphoreType.DMA((2, chunks)),
         ],
         compiler_params=pltpu.CompilerParams(vmem_limit_bytes=12 << 20),
-        cost_estimate=pl.CostEstimate(flops=4 * rows * cols, bytes_accessed=10 * rows * cols, transcendentals=0),
+        cost_estimate=pl.CostEstimate(flops=4 * rows * total, bytes_accessed=10 * rows * total, transcendentals=0),
         name="mix",
-    )(share, w, avg, *extra)
+    )(share, *arrays, *extra)
+
+
+def join_kernel(a_ref, b_ref, out_ref):
+    rows = a_ref.shape[0]
+    out_ref[pl.ds(0, rows), :] = a_ref[...]
+    out_ref[pl.ds(rows, b_ref.shape[0]), :] = b_ref[...]
+
+
+def joined(a, b):
+    shape = (a.shape[0] + b.shape[0], a.shape[1])
+    a, b = (pltpu.with_memory_space_constraint(x, pltpu.VMEM) for x in (a, b))
+    return pl.pallas_call(
+        join_kernel,
+        out_shape=pltpu.VMEM(shape, BF16),
+        in_specs=[VMEM, VMEM],
+        out_specs=VMEM,
+        compiler_params=pltpu.CompilerParams(vmem_limit_bytes=4 << 20),
+        cost_estimate=pl.CostEstimate(flops=shape[0] * shape[1], bytes_accessed=4 * shape[0] * shape[1], transcendentals=0),
+        name="join",
+    )(a, b)
 
 
 def place_kernel(counts, by, join, *refs):
@@ -86,7 +118,8 @@
         row = 0
         for _ in range(count):
             which, start, size, step, other = next(entries)
-            owner = lax.rem(chip + chips - step * sign, chips) * 2 + (1 - core if other else core)
+            side = other - 2 if other > 1 else 1 - core if other else core
+            owner = lax.rem(chip + chips - step * sign, chips) * 2 + side
             cols = pl.ds(pl.multiple_of(owner * width, width), width)
             piece = ref.at[pl.ds(row, size), :]
             row += size
@@ -175,13 +208,23 @@
     def place(outs, *arrays, join=0):
         return placed(outs, arrays, columns, rows, join)
 
-    def pieces(step, other, *which):
-        return tuple((w, 0, rows, step, other) for w in which)
-
-    (gate,) = mixed(mix_share, w_gate[0], avg_gate[0])
-    up, own = mixed(mix_share, w_up[0], avg_up[0], gate)
-    a1 = moved(gate, AHEAD)
-    a2 = moved(up, AHEAD)
+    def head(step, other):
+        return ((GATE, 0, rows, step, other), (UP, 0, HEAD, step, other))
+
+    def tail(step, other):
+        return ((UP, HEAD, rows - HEAD, step, other),)
+
+    (start,) = mixed(mix_share, ((w_gate[0], avg_gate[0], 0, FIRST),))
+    more, first = mixed(
+        mix_share,
+        ((w_gate[0], avg_gate[0], FIRST, rows - FIRST), (w_up[0], avg_up[0], 0, HEAD)),
+        start,
+    )
+    second, own = mixed(mix_share, ((w_up[0], avg_up[0], HEAD, rows - HEAD),), first)
+    a0 = moved(start, AHEAD)
+    a1 = moved(more, AHEAD)
+    a2 = moved(second, AHEAD)
+    a1 = joined(a0, a1)
     c1 = moved(a1, AHEAD)
     c2 = moved(a2, AHEAD)
     f1 = moved(c1, AHEAD)
@@ -194,16 +237,13 @@
     part = spread(part, ("y", "x")).reshape(-1, lanes)
     serve_router = ordered(part, nx * ny, nz).T
 
-    outs, _ = place(None, (own, pieces(0, 0, GATE, UP)))
-    outs, both = place(
-        outs, (a1, pieces(1, 0, GATE)), (a2, pieces(1, 0, UP)), (partner(own), pieces(0, 1, GATE, UP)), join=2
-    )
-    outs, _ = place(outs, (partner(both), pieces(1, 1, GATE, UP)))
-    outs, both = place(outs, (c1, pieces(2, 0, GATE)), (c2, pieces(2, 0, UP)), join=2)
-    both_other, f1_other, f2_other = partner(both), partner(f1), partner(f2)
-    outs, _ = place(outs, (both_other, pieces(2, 1, GATE, UP)), (f1, pieces(3, 0, GATE)))
-    outs, _ = place(outs, (f1_other, pieces(3, 1, GATE)), (f2, pieces(3, 0, UP)))
-    outs, _ = place(outs, (f2_other, pieces(3, 1, UP)))
+    outs, _ = place(None, (own, head(0, 0) + tail(0, 0)))
+    outs, both = place(outs, (a1, head(1, 0)), (a2, tail(1, 0)), (partner(own), head(0, 1) + tail(0, 1)), join=3)
+    outs, _ = place(outs, (partner(both), head(1, 1) + tail(1, 1)))
+    outs, both = place(outs, (c1, head(2, 0)), (c2, tail(2, 0)), join=3)
+    outs, _ = place(outs, (partner(both), head(2, 1) + tail(2, 1)), (f1, head(3, 0)), (partner(f1), head(3, 1)))
+    last = lax.all_gather(f2, "core", axis=0, tiled=True)
+    outs, _ = place(outs, (last, tail(3, 2) + tail(3, 3)))
     return outs[0][None], outs[1][None], serve_router
 
 

time: 138 us -> 126 us (0.913)
  blocking collectives: 33.6 us -> 15.9 us
  starting transfers between devices: 48.5 us -> 53.4 us
  Pallas kernels: 11.8 us -> 13.3 us
    all_to_all x2 -> x1, blocking collectives: 33.6 us -> 13 us  [spread(): lax.all_to_all(jnp.broadcast_to(x[None], (n, *x.shape)), axes, 0, 0, tile...]
    all_to_all x0 -> x1, starting transfers between devices: none -> 9.67 us  [spread(): lax.all_to_all(jnp.broadcast_to(x[None], (n, *x.shape)), axes, 0, 0, tile...]
    ppermute x6 -> x7, waiting for transfers between devices: 41.6 us -> 34.2 us  [moved(): return lax.ppermute(x, ('zlo', 'zhi'), pairs)]
    all_to_all x0 -> x1, waiting for transfers between devices: none -> 6.32 us  [spread(): lax.all_to_all(jnp.broadcast_to(x[None], (n, *x.shape)), axes, 0, 0, tile...]
    ppermute x5 -> x4, starting transfers between devices: 20.5 us -> 17.5 us  [partner(): return lax.ppermute(x, 'core', [(0, 1), (1, 0)])]
    all_gather x0 -> x1, blocking collectives: none -> 2.86 us  [local(): last = lax.all_gather(f2, 'core', axis=0, tiled=True)]
    ppermute x6 -> x7, starting transfers between devices: 28 us -> 26.3 us  [moved(): return lax.ppermute(x, ('zlo', 'zhi'), pairs)]
    pallas_call x2 -> x4, Pallas kernels: 3.4 us -> 4.43 us  [the longest x3 4.39 us: mixed(): pl.pallas_call(functools.partial(mix_kernel if extra else first_kernel, p...]
  transfers between devices with their start and end apart: 11 -> 12, of which waited for: 5 -> 5; matrix products, arithmetic and copies ran while one was open for 0% -> 1% of each run, Pallas kernels for 5% -> 4%
where the time goes in v3:
time: 126 us; the launch traced here: 125 us
  starting transfers between devices  53.4 us (42%)
  waiting for transfers between devices  40.6 us (32%)
  blocking collectives  15.9 us (13%)
  Pallas kernels  13.3 us (11%)
  between operations  1.5 us (1%)
    ppermute x7, waiting for transfers between devices, moved(): return lax.ppermute(x, ('zlo', 'zhi'), pairs)  34.2 us
    ppermute x7, starting transfers between devices, moved(): return lax.ppermute(x, ('zlo', 'zhi'), pairs)  26.3 us
    ppermute x4, starting transfers between devices, partner(): return lax.ppermute(x, 'core', [(0, 1), (1, 0)])  17.5 us
    all_to_all x1, blocking collectives, spread(): lax.all_to_all(jnp.broadcast_to(x[None], (n, *x.shape)), axes, 0, 0, tile...  13 us
    all_to_all x1, starting transfers between devices, spread(): lax.all_to_all(jnp.broadcast_to(x[None], (n, *x.shape)), axes, 0, 0, tile...  9.67 us
    pallas_call x6, Pallas kernels, placed(): pl.pallas_call(functools.partial(place_kernel, counts, by, join), out_sha...  7.78 us
    all_to_all x1, waiting for transfers between devices, spread(): lax.all_to_all(jnp.broadcast_to(x[None], (n, *x.shape)), axes, 0, 0, tile...  6.32 us
    pallas_call x3, Pallas kernels, mixed(): pl.pallas_call(functools.partial(mix_kernel if extra else first_kernel, p...  4.39 us
  transfers between devices with their start and end apart: 12, of which 5 were waited for; matrix products, arithmetic and copies ran while one was open for 1% of the time, Pallas kernels for 4%

profile of v3, /device:TPU:1, one launch (start us, length us, event | category | flops | bytes accessed | tf_op | source)
XLA Modules:
  0.0 125.4 jit_solution(9777426592077480621)
XLA Ops:
  1.3 1.3 %mix.3.refs_4_ = bf16[512,256]{1,0:T(8,128)(2,1)S(1)} custom-call(f32[1]{0:T(128)S(6)} %copy.30.refs_0_.share_ref, f32[256,1024]{1,0:T(8,128)} %bitcast.14, f32[256,1024]{1,0:T(8,128)} %bitcast.16), custom_call_target="tpu_custom_call" | custom-call | flops 524288 | bytes 1310720 | tf_op jit(solution)/shard_map/mix/pallas_call | solution.py:71
  2.6 1.5 %mix.4 = (bf16[768,256]{1,0:T(8,128)(2,1)S(1)}, bf16[1280,256]{1,0:T(8,128)(2,1)S(1)}) custom-call(f32[1]{0:T(128)S(6)} %copy.30.refs_0_.share_ref, f32[256,1024]{1,0:T(8,128)} %bitcast.15, f32[256,1024]{1,0:T(8,128)} %bitcast.17, f32[256,1024]{1,0:T(8,128)} %bitcast.18, f32[256,1024]{1,0:T(8,128)} %bitcast.20, bf16[512,256]{1,0:T(8,128)(2,1)S(1)} %mix.3.refs_4_), custom_call_target="tpu_custom_call" | custom-call | flops 786432 | bytes 1966080 | tf_op jit(solution)/shard_map/mix/pallas_call | solution.py:71
  4.1 1.5 %mix.5 = (bf16[768,256]{1,0:T(8,128)(2,1)S(1)}, bf16[2048,256]{1,0:T(8,128)(2,1)S(1)}) custom-call(f32[1]{0:T(128)S(6)} %copy.30.refs_0_.share_ref, f32[256,1024]{1,0:T(8,128)} %bitcast.19, f32[256,1024]{1,0:T(8,128)} %bitcast.21, bf16[1280,256]{1,0:T(8,128)(2,1)S(1)} %get-tuple-element.21.refs_2_), custom_call_target="tpu_custom_call" | custom-call | flops 786432 | bytes 1966080 | tf_op jit(solution)/shard_map/mix/pallas_call | solution.py:71
  5.7 8.7 %collective-permute-start.6 = (bf16[2048,256]{1,0:T(8,128)(2,1)S(1)}, bf16[2048,256]{1,0:T(8,128)(2,1)S(1)}, u32[]{:S(2)}, u32[]{:S(2)}) collective-permute-start(bf16[2048,256]{1,0:T(8,128)(2,1)S(1)} %get-tuple-element.24.refs_0_), channel_id=1, source_target_pairs={{0,1},{1,0},{2,3},{3,2},{4,5},{5,4},{6,7},{7,6},{8,9},{9,8},{10,11... | collective-permute-start | bytes 3145736 | tf_op jit(solution)/shard_map/ppermute | solution.py:206
  14.4 5.3 %collective-permute-start.4 = (bf16[768,256]{1,0:T(8,128)(2,1)S(1)}, bf16[768,256]{1,0:T(8,128)(2,1)S(1)}, u32[]{:S(2)}, u32[]{:S(2)}) collective-permute-start(bf16[768,256]{1,0:T(8,128)(2,1)S(1)} %get-tuple-element.23), channel_id=1, source_target_pairs={{0,6},{2,0},{4,2},{6,4},{256,258},{258,260},{260,262},{262,256},{1... | collective-permute-start | bytes 1179656 | tf_op jit(solution)/shard_map/ppermute | solution.py:203
  19.8 2.2 %collective-permute-start = (bf16[768,256]{1,0:T(8,128)(2,1)S(1)}, bf16[768,256]{1,0:T(8,128)(2,1)S(1)}, u32[]{:S(2)}, u32[]{:S(2)}) collective-permute-start(bf16[768,256]{1,0:T(8,128)(2,1)S(1)} %get-tuple-element.22), channel_id=1, source_target_pairs={{0,6},{2,0},{4,2},{6,4},{256,258},{258,260},{260,262},{262,256},{1... | collective-permute-start | bytes 1179656 | tf_op jit(solution)/shard_map/ppermute | solution.py:203
  21.9 1.9 %collective-permute-start.3 = (bf16[512,256]{1,0:T(8,128)(2,1)S(1)}, bf16[512,256]{1,0:T(8,128)(2,1)S(1)}, u32[]{:S(2)}, u32[]{:S(2)}) collective-permute-start(bf16[512,256]{1,0:T(8,128)(2,1)S(1)} %mix.3.refs_4_), channel_id=1, source_target_pairs={{0,6},{2,0},{4,2},{6,4},{256,258},{258,260},{260,262},{262,256},{1... | collective-permute-start | bytes 786440 | tf_op jit(solution)/shard_map/ppermute | solution.py:203
  23.9 1.0 place.6
  24.9 17.4 %collective-permute-done.3.a_ref = bf16[512,256]{1,0:T(8,128)(2,1)S(1)} collective-permute-done((bf16[512,256]{1,0:T(8,128)(2,1)S(1)}, bf16[512,256]{1,0:T(8,128)(2,1)S(1)}, u32[]{:S(2)}, u32[]{:S(2)}) %collective-permute-start.3) | collective-permute-done | bytes 262176 | tf_op jit(solution)/shard_map/ppermute | solution.py:203
  42.2 0.0 collective-permute-done.4.b_ref
  42.3 0.0 collective-permute-done.refs_1_
  42.3 0.0 collective-permute-done.6.refs_2_
  42.3 1.4 %place.7 = (bf16[1024,2048]{1,0:T(8,128)(2,1)}, bf16[1024,2048]{1,0:T(8,128)(2,1)}, bf16[2048,256]{1,0:T(8,128)(2,1)S(1)}) custom-call(bf16[1280,256]{1,0:T(8,128)(2,1)S(1)} %join.1.refs_0_, bf16[768,256]{1,0:T(8,128)(2,1)S(1)} %collective-permute-done.refs_1_, ...), custom_call_target="tpu_custom_call", output_to_operand_aliasing={{0}: (3, {}), {1}: (4, {})} | custom-call | flops 2097152 | bytes 4194304 | tf_op jit(solution)/shard_map/place/pallas_call | solution.py:148
  43.7 2.8 %collective-permute-start.7 = (bf16[2048,256]{1,0:T(8,128)(2,1)S(1)}, bf16[2048,256]{1,0:T(8,128)(2,1)S(1)}, u32[]{:S(2)}, u32[]{:S(2)}) collective-permute-start(bf16[2048,256]{1,0:T(8,128)(2,1)S(1)} %get-tuple-element.27), channel_id=1, source_target_pairs={{0,1},{1,0},{2,3},{3,2},{4,5},{5,4},{6,7},{7,6},{8,9},{9,8},{10,11... | collective-permute-start | bytes 3145736 | tf_op jit(solution)/shard_map/ppermute | solution.py:206
  46.5 6.2 %collective-permute-start.5 = (bf16[1280,256]{1,0:T(8,128)(2,1)S(1)}, bf16[1280,256]{1,0:T(8,128)(2,1)S(1)}, u32[]{:S(2)}, u32[]{:S(2)}) collective-permute-start(bf16[1280,256]{1,0:T(8,128)(2,1)S(1)} %join.1.refs_0_), channel_id=1, source_target_pairs={{0,6},{2,0},{4,2},{6,4},{256,258},{258,260},{260,262},{262,256},{1... | collective-permute-start | bytes 1966088 | tf_op jit(solution)/shard_map/ppermute | solution.py:203
  52.7 1.9 %collective-permute-start.1 = (bf16[768,256]{1,0:T(8,128)(2,1)S(1)}, bf16[768,256]{1,0:T(8,128)(2,1)S(1)}, u32[]{:S(2)}, u32[]{:S(2)}) collective-permute-start(bf16[768,256]{1,0:T(8,128)(2,1)S(1)} %collective-permute-done.refs_1_), channel_id=1, source_target_pairs={{0,6},{2,0},{4,2},{6,4},{256,258},{258,260},{260,262},{262,256},{1... | collective-permute-start | bytes 1179656 | tf_op jit(solution)/shard_map/ppermute | solution.py:203
  54.7 12.1 %collective-permute-done.5.refs_0_ = bf16[1280,256]{1,0:T(8,128)(2,1)S(1)} collective-permute-done((bf16[1280,256]{1,0:T(8,128)(2,1)S(1)}, bf16[1280,256]{1,0:T(8,128)(2,1)S(1)}, u32[]{:S(2)}, u32[]{:S(2)}) %collective-permute-start.5) | collective-permute-done | bytes 655392 | tf_op jit(solution)/shard_map/ppermute | solution.py:203
  66.8 6.2 %collective-permute-start.9 = (bf16[1280,256]{1,0:T(8,128)(2,1)S(1)}, bf16[1280,256]{1,0:T(8,128)(2,1)S(1)}, u32[]{:S(2)}, u32[]{:S(2)}) collective-permute-start(bf16[1280,256]{1,0:T(8,128)(2,1)S(1)} %collective-permute-done.5.refs_0_), channel_id=1, source_target_pairs={{0,6},{2,0},{4,2},{6,4},{256,258},{258,260},{260,262},{262,256},{1... | collective-permute-start | bytes 1966088 | tf_op jit(solution)/shard_map/ppermute | solution.py:203
  73.0 0.0 collective-permute-done.7.refs_0_
  73.0 1.0 place.8
  74.0 1.2 collective-permute-done.1.refs_1_
  75.2 0.0 copy-start
  75.2 0.0 copy-start.1
  75.2 2.0 %place.9 = (bf16[1024,2048]{1,0:T(8,128)(2,1)}, bf16[1024,2048]{1,0:T(8,128)(2,1)}, bf16[2048,256]{1,0:T(8,128)(2,1)}) custom-call(bf16[1280,256]{1,0:T(8,128)(2,1)S(1)} %collective-permute-done.5.refs_0_, bf16[768,256]{1,0:T(8,128)(2,1)S(1)} %collective-permute-done.1.refs_1_, ...), custom_call_target="tpu_custom_call", output_to_operand_aliasing={{0}: (2, {}), {1}: (3, {})} | custom-call | flops 1048576 | bytes 2097152 | tf_op jit(solution)/shard_map/place/pallas_call | solution.py:148
  77.2 3.3 %collective-permute-start.8 = (bf16[2048,256]{1,0:T(8,128)(2,1)}, bf16[2048,256]{1,0:T(8,128)(2,1)S(1)}, u32[]{:S(2)}, u32[]{:S(2)}) collective-permute-start(bf16[2048,256]{1,0:T(8,128)(2,1)} %get-tuple-element.32), channel_id=1, source_target_pairs={{0,1},{1,0},{2,3},{3,2},{4,5},{5,4},{6,7},{7,6},{8,9},{9,8},{10,11... | collective-permute-start | bytes 3145736 | tf_op jit(solution)/shard_map/ppermute | solution.py:206
  80.5 0.0 copy-done
  80.5 0.0 copy-done.1
  80.5 13.0 %all_to_all.10 = bf16[16,2,128]{2,1,0:T(2,128)(2,1)S(1)} all-to-all(bf16[16,2,128]{2,1,0:T(2,128)(2,1)S(1)} %broadcast_in_dim.27), channel_id=1, replica_groups=mesh['zlo'=2,'y'=8,'x'=4,'zhi'=4,'core'=2] {'zlo','zhi','core'}, dimensions={0} | all-to-all | bytes 16384 | tf_op jit(solution)/shard_map/all_to_all | solution.py:191
  93.6 0.7 broadcast_in_dim.29
  94.3 9.7 %all-to-all-start.1 = ((bf16[32,32,128]{2,1,0:T(8,128)(2,1)}), bf16[32,32,128]{2,1,0:T(8,128)(2,1)S(1)}, u32[]{:S(2)}, u32[]{:S(2)}) async-start(bf16[32,32,128]{2,1,0:T(8,128)(2,1)} %broadcast_in_dim.29), calls=%async_computation.1 | async-start | bytes 524288 | tf_op jit(solution)/shard_map/all_to_all | solution.py:191
  104.0 0.0 collective-permute-done.9.refs_1_
  104.0 2.7 %collective-permute-start.10 = (bf16[1280,256]{1,0:T(8,128)(2,1)S(1)}, bf16[1280,256]{1,0:T(8,128)(2,1)S(1)}, u32[]{:S(2)}, u32[]{:S(2)}) collective-permute-start(bf16[1280,256]{1,0:T(8,128)(2,1)S(1)} %collective-permute-done.9.refs_1_), channel_id=1, source_target_pairs={{0,1},{1,0},{2,3},{3,2},{4,5},{5,4},{6,7},{7,6},{8,9},{9,8},{10,11... | collective-permute-start | bytes 1966088 | tf_op jit(solution)/shard_map/ppermute | solution.py:206
  106.7 2.5 %collective-permute-start.2 = (bf16[768,256]{1,0:T(8,128)(2,1)S(1)}, bf16[768,256]{1,0:T(8,128)(2,1)S(1)}, u32[]{:S(2)}, u32[]{:S(2)}) collective-permute-start(bf16[768,256]{1,0:T(8,128)(2,1)S(1)} %collective-permute-done.1.refs_1_), channel_id=1, source_target_pairs={{0,6},{2,0},{4,2},{6,4},{256,258},{258,260},{260,262},{262,256},{1... | collective-permute-start | bytes 1179656 | tf_op jit(solution)/shard_map/ppermute | solution.py:203
  109.2 6.3 %all-to-all-done.1 = bf16[32,32,128]{2,1,0:T(8,128)(2,1)S(1)} async-done(((bf16[32,32,128]{2,1,0:T(8,128)(2,1)}), bf16[32,32,128]{2,1,0:T(8,128)(2,1)S(1)}, u32[]{:S(2)}, u32[]{:S(2)}) %all-to-all-start.1) | async-done | bytes 262176 | tf_op jit(solution)/shard_map/all_to_all | solution.py:191
  115.5 1.0 order.1
  116.6 3.5 %collective-permute-done.2 = bf16[768,256]{1,0:T(8,128)(2,1)S(1)} collective-permute-done((bf16[768,256]{1,0:T(8,128)(2,1)S(1)}, bf16[768,256]{1,0:T(8,128)(2,1)S(1)}, u32[]{:S(2)}, u32[]{:S(2)}) %collective-permute-start.2) | collective-permute-done | bytes 393248 | tf_op jit(solution)/shard_map/ppermute | solution.py:203
  120.1 2.9 %all_gather.3.refs_0_ = bf16[1536,256]{1,0:T(8,128)(2,1)S(1)} all-gather(bf16[768,256]{1,0:T(8,128)(2,1)S(1)} %collective-permute-done.2), channel_id=1, replica_groups=mesh['zlo'=2,'y'=8,'x'=4,'zhi'=4,'core'=2] {'core'}, dimensions={0}, use_global_device_ids=true | all-gather | bytes 1179648 | tf_op jit(solution)/shard_map/all_gather | solution.py:245
  123.0 0.0 collective-permute-done.10.refs_2_
  123.0 0.0 collective-permute-done.8.refs_0_
  123.0 1.4 %place.10 = (bf16[1024,2048]{1,0:T(8,128)(2,1)}, bf16[1024,2048]{1,0:T(8,128)(2,1)}) custom-call(bf16[2048,256]{1,0:T(8,128)(2,1)S(1)} %collective-permute-done.8.refs_0_, bf16[1280,256]{1,0:T(8,128)(2,1)S(1)} %collective-permute-done.9.refs_1_, bf16[1280,256]{1,0:T(8,128)(2,1)S(1)} %collective-permute-done.10.refs_2_, ...), custom_call_target="tpu_custom_call", output_to_operand_aliasing={{0}: (3, {}), {1}: (4, {})} | custom-call | flops 2359296 | bytes 4718592 | tf_op jit(solution)/shard_map/place/pallas_call | solution.py:148
  124.4 0.9 place.11
  (3 shorter events, 0.1 us)
Async XLA Ops:
  5.7 36.6 %collective-permute-start.6 = (bf16[2048,256]{1,0:T(8,128)(2,1)S(1)}, bf16[2048,256]{1,0:T(8,128)(2,1)S(1)}, u32[]{:S(2)}, u32[]{:S(2)}) collective-permute-start(bf16[2048,256]{1,0:T(8,128)(2,1)S(1)} %get-tuple-element.24.refs_0_), channel_id=1, source_target_pairs={{0,1},{1,0},{2,3},{3,2},{4,5},{5,4},{6,7},{7,6},{8,9},{9,8},{10,11... | collective-permute-start | bytes 3145736 | tf_op jit(solution)/shard_map/ppermute | solution.py:206
  14.4 27.8 %collective-permute-start.4 = (bf16[768,256]{1,0:T(8,128)(2,1)S(1)}, bf16[768,256]{1,0:T(8,128)(2,1)S(1)}, u32[]{:S(2)}, u32[]{:S(2)}) collective-permute-start(bf16[768,256]{1,0:T(8,128)(2,1)S(1)} %get-tuple-element.23), channel_id=1, source_target_pairs={{0,6},{2,0},{4,2},{6,4},{256,258},{258,260},{260,262},{262,256},{1... | collective-permute-start | bytes 1179656 | tf_op jit(solution)/shard_map/ppermute | solution.py:203
  19.8 22.5 %collective-permute-start = (bf16[768,256]{1,0:T(8,128)(2,1)S(1)}, bf16[768,256]{1,0:T(8,128)(2,1)S(1)}, u32[]{:S(2)}, u32[]{:S(2)}) collective-permute-start(bf16[768,256]{1,0:T(8,128)(2,1)S(1)} %get-tuple-element.22), channel_id=1, source_target_pairs={{0,6},{2,0},{4,2},{6,4},{256,258},{258,260},{260,262},{262,256},{1... | collective-permute-start | bytes 1179656 | tf_op jit(solution)/shard_map/ppermute | solution.py:203
  21.9 20.3 %collective-permute-start.3 = (bf16[512,256]{1,0:T(8,128)(2,1)S(1)}, bf16[512,256]{1,0:T(8,128)(2,1)S(1)}, u32[]{:S(2)}, u32[]{:S(2)}) collective-permute-start(bf16[512,256]{1,0:T(8,128)(2,1)S(1)} %mix.3.refs_4_), channel_id=1, source_target_pairs={{0,6},{2,0},{4,2},{6,4},{256,258},{258,260},{260,262},{262,256},{1... | collective-permute-start | bytes 786440 | tf_op jit(solution)/shard_map/ppermute | solution.py:203
  43.7 29.3 %collective-permute-start.7 = (bf16[2048,256]{1,0:T(8,128)(2,1)S(1)}, bf16[2048,256]{1,0:T(8,128)(2,1)S(1)}, u32[]{:S(2)}, u32[]{:S(2)}) collective-permute-start(bf16[2048,256]{1,0:T(8,128)(2,1)S(1)} %get-tuple-element.27), channel_id=1, source_target_pairs={{0,1},{1,0},{2,3},{3,2},{4,5},{5,4},{6,7},{7,6},{8,9},{9,8},{10,11... | collective-permute-start | bytes 3145736 | tf_op jit(solution)/shard_map/ppermute | solution.py:206
  46.5 20.3 %collective-permute-start.5 = (bf16[1280,256]{1,0:T(8,128)(2,1)S(1)}, bf16[1280,256]{1,0:T(8,128)(2,1)S(1)}, u32[]{:S(2)}, u32[]{:S(2)}) collective-permute-start(bf16[1280,256]{1,0:T(8,128)(2,1)S(1)} %join.1.refs_0_), channel_id=1, source_target_pairs={{0,6},{2,0},{4,2},{6,4},{256,258},{258,260},{260,262},{262,256},{1... | collective-permute-start | bytes 1966088 | tf_op jit(solution)/shard_map/ppermute | solution.py:203
  52.7 22.5 %collective-permute-start.1 = (bf16[768,256]{1,0:T(8,128)(2,1)S(1)}, bf16[768,256]{1,0:T(8,128)(2,1)S(1)}, u32[]{:S(2)}, u32[]{:S(2)}) collective-permute-start(bf16[768,256]{1,0:T(8,128)(2,1)S(1)} %collective-permute-done.refs_1_), channel_id=1, source_target_pairs={{0,6},{2,0},{4,2},{6,4},{256,258},{258,260},{260,262},{262,256},{1... | collective-permute-start | bytes 1179656 | tf_op jit(solution)/shard_map/ppermute | solution.py:203
  66.8 37.2 %collective-permute-start.9 = (bf16[1280,256]{1,0:T(8,128)(2,1)S(1)}, bf16[1280,256]{1,0:T(8,128)(2,1)S(1)}, u32[]{:S(2)}, u32[]{:S(2)}) collective-permute-start(bf16[1280,256]{1,0:T(8,128)(2,1)S(1)} %collective-permute-done.5.refs_0_), channel_id=1, source_target_pairs={{0,6},{2,0},{4,2},{6,4},{256,258},{258,260},{260,262},{262,256},{1... | collective-permute-start | bytes 1966088 | tf_op jit(solution)/shard_map/ppermute | solution.py:203
  75.2 5.3 %copy-start = (f32[256,1]{0,1:T(1,128)S(1)}, f32[256,1]{0,1:T(1,128)}, u32[]{:S(2)}) copy-start(f32[256,1]{0,1:T(1,128)} %param.12) | copy-start | bytes 3076
  75.2 5.3 %copy-start.1 = (f32[256]{0:T(256)S(1)}, f32[256]{0:T(256)}, u32[]{:S(2)}) copy-start(f32[256]{0:T(256)} %param.13) | copy-start | bytes 3076
  77.2 45.8 %collective-permute-start.8 = (bf16[2048,256]{1,0:T(8,128)(2,1)}, bf16[2048,256]{1,0:T(8,128)(2,1)S(1)}, u32[]{:S(2)}, u32[]{:S(2)}) collective-permute-start(bf16[2048,256]{1,0:T(8,128)(2,1)} %get-tuple-element.32), channel_id=1, source_target_pairs={{0,1},{1,0},{2,3},{3,2},{4,5},{5,4},{6,7},{7,6},{8,9},{9,8},{10,11... | collective-permute-start | bytes 3145736 | tf_op jit(solution)/shard_map/ppermute | solution.py:206
  94.3 21.2 %all-to-all-start.1 = ((bf16[32,32,128]{2,1,0:T(8,128)(2,1)}), bf16[32,32,128]{2,1,0:T(8,128)(2,1)S(1)}, u32[]{:S(2)}, u32[]{:S(2)}) async-start(bf16[32,32,128]{2,1,0:T(8,128)(2,1)} %broadcast_in_dim.29), calls=%async_computation.1 | async-start | bytes 524288 | tf_op jit(solution)/shard_map/all_to_all | solution.py:191
  104.0 19.0 %collective-permute-start.10 = (bf16[1280,256]{1,0:T(8,128)(2,1)S(1)}, bf16[1280,256]{1,0:T(8,128)(2,1)S(1)}, u32[]{:S(2)}, u32[]{:S(2)}) collective-permute-start(bf16[1280,256]{1,0:T(8,128)(2,1)S(1)} %collective-permute-done.9.refs_1_), channel_id=1, source_target_pairs={{0,1},{1,0},{2,3},{3,2},{4,5},{5,4},{6,7},{7,6},{8,9},{9,8},{10,11... | collective-permute-start | bytes 1966088 | tf_op jit(solution)/shard_map/ppermute | solution.py:206
  106.7 13.5 %collective-permute-start.2 = (bf16[768,256]{1,0:T(8,128)(2,1)S(1)}, bf16[768,256]{1,0:T(8,128)(2,1)S(1)}, u32[]{:S(2)}, u32[]{:S(2)}) collective-permute-start(bf16[768,256]{1,0:T(8,128)(2,1)S(1)} %collective-permute-done.1.refs_1_), channel_id=1, source_target_pairs={{0,6},{2,0},{4,2},{6,4},{256,258},{258,260},{260,262},{262,256},{1... | collective-permute-start | bytes 1179656 | tf_op jit(solution)/shard_map/ppermute | solution.py:203

commit v4 on v3

--- a/solution.py
+++ b/solution.py
@@ -20,7 +20,7 @@
 VMEM = pl.BlockSpec(memory_space=pltpu.VMEM)
 SMEM = pl.BlockSpec(memory_space=pltpu.SMEM)
 GATE, UP = 0, 1
-AHEAD = -1
+AHEAD = 1
 
 
 def mix_kernel(plan, share_ref, *refs):
@@ -238,10 +238,22 @@
     serve_router = ordered(part, nx * ny, nz).T
 
     outs, _ = place(None, (own, head(0, 0) + tail(0, 0)))
-    outs, both = place(outs, (a1, head(1, 0)), (a2, tail(1, 0)), (partner(own), head(0, 1) + tail(0, 1)), join=3)
-    outs, _ = place(outs, (partner(both), head(1, 1) + tail(1, 1)))
-    outs, both = place(outs, (c1, head(2, 0)), (c2, tail(2, 0)), join=3)
-    outs, _ = place(outs, (partner(both), head(2, 1) + tail(2, 1)), (f1, head(3, 0)), (partner(f1), head(3, 1)))
+    d0 = partner(own)
+    both = joined(a1, a2)
+    d1 = partner(both)
+    outs, _ = place(
+        outs, (a1, head(1, 0)), (a2, tail(1, 0)), (d0, head(0, 1) + tail(0, 1)), (d1, head(1, 1) + tail(1, 1))
+    )
+    both = joined(c1, c2)
+    d2 = partner(both)
+    outs, _ = place(
+        outs,
+        (c1, head(2, 0)),
+        (c2, tail(2, 0)),
+        (d2, head(2, 1) + tail(2, 1)),
+        (f1, head(3, 0)),
+        (partner(f1), head(3, 1)),
+    )
     last = lax.all_gather(f2, "core", axis=0, tiled=True)
     outs, _ = place(outs, (last, tail(3, 2) + tail(3, 3)))
     return outs[0][None], outs[1][None], serve_router

time: 126 us -> 130 us (1.032)
  Pallas kernels: 13.3 us -> 18 us
  waiting for transfers between devices: 40.6 us -> 37.8 us
  starting transfers between devices: 53.4 us -> 55.5 us
    ppermute x7, starting transfers between devices: 26.3 us -> 31.6 us  [moved(): return lax.ppermute(x, ('zlo', 'zhi'), pairs)]
    ppermute x4, starting transfers between devices: 17.5 us -> 14.2 us  [partner(): return lax.ppermute(x, 'core', [(0, 1), (1, 0)])]
    all_to_all x1, waiting for transfers between devices: 6.32 us -> 4.01 us  [spread(): lax.all_to_all(jnp.broadcast_to(x[None], (n, *x.shape)), axes, 0, 0, tile...]
    pallas_call x1 -> x3, Pallas kernels: 0.04 us -> 2.13 us  [joined(): pl.pallas_call(join_kernel, out_shape=pltpu.VMEM(shape, BF16), in_specs=[...]
    pallas_call x6 -> x4, Pallas kernels: 7.78 us -> 9.5 us  [placed(): pl.pallas_call(functools.partial(place_kernel, counts, by, join), out_sha...]
  transfers between devices with their start and end apart: 12 -> 12, of which waited for: 5 -> 4; matrix products, arithmetic and copies ran while one was open for 1% -> 1% of each run, Pallas kernels for 4% -> 9%
where the time goes in v4:
time: 130 us; the launch traced here: 129 us
  starting transfers between devices  55.5 us (43%)
  waiting for transfers between devices  37.8 us (29%)
  Pallas kernels  18 us (14%)
  blocking collectives  15.3 us (12%)
  between operations  1.5 us (1%)
    ppermute x7, waiting for transfers between devices, moved(): return lax.ppermute(x, ('zlo', 'zhi'), pairs)  33.8 us
    ppermute x7, starting transfers between devices, moved(): return lax.ppermute(x, ('zlo', 'zhi'), pairs)  31.6 us
    ppermute x4, starting transfers between devices, partner(): return lax.ppermute(x, 'core', [(0, 1), (1, 0)])  14.2 us
    all_to_all x1, blocking collectives, spread(): lax.all_to_all(jnp.broadcast_to(x[None], (n, *x.shape)), axes, 0, 0, tile...  12.3 us
    all_to_all x1, starting transfers between devices, spread(): lax.all_to_all(jnp.broadcast_to(x[None], (n, *x.shape)), axes, 0, 0, tile...  9.67 us
    pallas_call x4, Pallas kernels, placed(): pl.pallas_call(functools.partial(place_kernel, counts, by, join), out_sha...  9.5 us
    pallas_call x3, Pallas kernels, mixed(): pl.pallas_call(functools.partial(mix_kernel if extra else first_kernel, p...  5.33 us
    all_to_all x1, waiting for transfers between devices, spread(): lax.all_to_all(jnp.broadcast_to(x[None], (n, *x.shape)), axes, 0, 0, tile...  4.01 us
  transfers between devices with their start and end apart: 12, of which 4 were waited for; matrix products, arithmetic and copies ran while one was open for 1% of the time, Pallas kernels for 9%

profile of v4, /device:TPU:1, one launch (start us, length us, event | category | flops | bytes accessed | tf_op | source)
XLA Modules:
  0.0 128.9 jit_solution(17270516581299900935)
XLA Ops:
  1.3 1.3 %mix.3.refs_4_ = bf16[512,256]{1,0:T(8,128)(2,1)S(1)} custom-call(f32[1]{0:T(128)S(6)} %copy.22.refs_0_.share_ref, f32[256,1024]{1,0:T(8,128)} %bitcast.14, f32[256,1024]{1,0:T(8,128)} %bitcast.16), custom_call_target="tpu_custom_call" | custom-call | flops 524288 | bytes 1310720 | tf_op jit(solution)/shard_map/mix/pallas_call | solution.py:71
  2.6 1.5 %mix.4 = (bf16[768,256]{1,0:T(8,128)(2,1)S(1)}, bf16[1280,256]{1,0:T(8,128)(2,1)S(1)}) custom-call(f32[1]{0:T(128)S(6)} %copy.22.refs_0_.share_ref, f32[256,1024]{1,0:T(8,128)} %bitcast.15, f32[256,1024]{1,0:T(8,128)} %bitcast.17, f32[256,1024]{1,0:T(8,128)} %bitcast.18, f32[256,1024]{1,0:T(8,128)} %bitcast.20, bf16[512,256]{1,0:T(8,128)(2,1)S(1)} %mix.3.refs_4_), custom_call_target="tpu_custom_call" | custom-call | flops 786432 | bytes 1966080 | tf_op jit(solution)/shard_map/mix/pallas_call | solution.py:71
  4.1 0.0 copy-start
  4.1 0.0 copy-start.1
  4.2 6.6 %collective-permute-start.4 = (bf16[768,256]{1,0:T(8,128)(2,1)S(1)}, bf16[768,256]{1,0:T(8,128)(2,1)S(1)}, u32[]{:S(2)}, u32[]{:S(2)}) collective-permute-start(bf16[768,256]{1,0:T(8,128)(2,1)S(1)} %get-tuple-element.17), channel_id=1, source_target_pairs={{0,2},{2,4},{4,6},{6,0},{256,262},{258,256},{260,258},{262,260},{1... | collective-permute-start | bytes 1179656 | tf_op jit(solution)/shard_map/ppermute | solution.py:203
  10.8 7.0 %collective-permute-start.3 = (bf16[512,256]{1,0:T(8,128)(2,1)S(1)}, bf16[512,256]{1,0:T(8,128)(2,1)S(1)}, u32[]{:S(2)}, u32[]{:S(2)}) collective-permute-start(bf16[512,256]{1,0:T(8,128)(2,1)S(1)} %mix.3.refs_4_), channel_id=1, source_target_pairs={{0,2},{2,4},{4,6},{6,0},{256,262},{258,256},{260,258},{262,260},{1... | collective-permute-start | bytes 786440 | tf_op jit(solution)/shard_map/ppermute | solution.py:203
  17.8 11.8 %collective-permute-done.3.a_ref = bf16[512,256]{1,0:T(8,128)(2,1)S(1)} collective-permute-done((bf16[512,256]{1,0:T(8,128)(2,1)S(1)}, bf16[512,256]{1,0:T(8,128)(2,1)S(1)}, u32[]{:S(2)}, u32[]{:S(2)}) %collective-permute-start.3) | collective-permute-done | bytes 262176 | tf_op jit(solution)/shard_map/ppermute | solution.py:203
  29.6 0.0 collective-permute-done.4.b_ref
  29.7 1.9 %collective-permute-start.5 = (bf16[1280,256]{1,0:T(8,128)(2,1)S(1)}, bf16[1280,256]{1,0:T(8,128)(2,1)S(1)}, u32[]{:S(2)}, u32[]{:S(2)}) collective-permute-start(bf16[1280,256]{1,0:T(8,128)(2,1)S(1)} %join.3.a_ref.refs_0_), channel_id=1, source_target_pairs={{0,2},{2,4},{4,6},{6,0},{256,262},{258,256},{260,258},{262,260},{1... | collective-permute-start | bytes 1966088 | tf_op jit(solution)/shard_map/ppermute | solution.py:203
  31.6 2.5 %mix.5 = (bf16[768,256]{1,0:T(8,128)(2,1)S(1)}, bf16[2048,256]{1,0:T(8,128)(2,1)}) custom-call(f32[1]{0:T(128)S(6)} %copy.22.refs_0_.share_ref, f32[256,1024]{1,0:T(8,128)} %bitcast.19, f32[256,1024]{1,0:T(8,128)} %bitcast.21, bf16[1280,256]{1,0:T(8,128)(2,1)S(1)} %get-tuple-element.15.refs_2_), custom_call_target="tpu_custom_call" | custom-call | flops 786432 | bytes 1966080 | tf_op jit(solution)/shard_map/mix/pallas_call | solution.py:71
  34.1 5.9 %collective-permute-start = (bf16[768,256]{1,0:T(8,128)(2,1)S(1)}, bf16[768,256]{1,0:T(8,128)(2,1)S(1)}, u32[]{:S(2)}, u32[]{:S(2)}) collective-permute-start(bf16[768,256]{1,0:T(8,128)(2,1)S(1)} %get-tuple-element.16), channel_id=1, source_target_pairs={{0,2},{2,4},{4,6},{6,0},{256,262},{258,256},{260,258},{262,260},{1... | collective-permute-start | bytes 1179656 | tf_op jit(solution)/shard_map/ppermute | solution.py:203
  40.0 16.7 %collective-permute-done.b_ref.refs_1_ = bf16[768,256]{1,0:T(8,128)(2,1)S(1)} collective-permute-done((bf16[768,256]{1,0:T(8,128)(2,1)S(1)}, bf16[768,256]{1,0:T(8,128)(2,1)S(1)}, u32[]{:S(2)}, u32[]{:S(2)}) %collective-permute-start) | collective-permute-done | bytes 393248 | tf_op jit(solution)/shard_map/ppermute | solution.py:203
  56.7 1.9 %collective-permute-start.1 = (bf16[768,256]{1,0:T(8,128)(2,1)S(1)}, bf16[768,256]{1,0:T(8,128)(2,1)S(1)}, u32[]{:S(2)}, u32[]{:S(2)}) collective-permute-start(bf16[768,256]{1,0:T(8,128)(2,1)S(1)} %collective-permute-done.b_ref.refs_1_), channel_id=1, source_target_pairs={{0,2},{2,4},{4,6},{6,0},{256,262},{258,256},{260,258},{262,260},{1... | collective-permute-start | bytes 1179656 | tf_op jit(solution)/shard_map/ppermute | solution.py:203
  58.6 0.0 collective-permute-done.5.a_ref.refs_0_
  58.6 6.1 %collective-permute-start.7 = (bf16[1280,256]{1,0:T(8,128)(2,1)S(1)}, bf16[1280,256]{1,0:T(8,128)(2,1)}, u32[]{:S(2)}, u32[]{:S(2)}) collective-permute-start(bf16[1280,256]{1,0:T(8,128)(2,1)S(1)} %collective-permute-done.5.a_ref.refs_0_), channel_id=1, source_target_pairs={{0,2},{2,4},{4,6},{6,0},{256,262},{258,256},{260,258},{262,260},{1... | collective-permute-start | bytes 1966088 | tf_op jit(solution)/shard_map/ppermute | solution.py:203
  64.7 4.9 %collective-permute-start.9 = (bf16[2048,256]{1,0:T(8,128)(2,1)}, bf16[2048,256]{1,0:T(8,128)(2,1)}, u32[]{:S(2)}, u32[]{:S(2)}) collective-permute-start(bf16[2048,256]{1,0:T(8,128)(2,1)} %get-tuple-element.18.refs_0_), channel_id=1, source_target_pairs={{0,1},{1,0},{2,3},{3,2},{4,5},{5,4},{6,7},{7,6},{8,9},{9,8},{10,11... | collective-permute-start | bytes 3145736 | tf_op jit(solution)/shard_map/ppermute | solution.py:206
  69.5 1.0 join.5
  70.6 1.9 %collective-permute-start.10 = (bf16[2048,256]{1,0:T(8,128)(2,1)}, bf16[2048,256]{1,0:T(8,128)(2,1)}, u32[]{:S(2)}, u32[]{:S(2)}) collective-permute-start(bf16[2048,256]{1,0:T(8,128)(2,1)} %join.5), channel_id=1, source_target_pairs={{0,1},{1,0},{2,3},{3,2},{4,5},{5,4},{6,7},{7,6},{8,9},{9,8},{10,11... | collective-permute-start | bytes 3145736 | tf_op jit(solution)/shard_map/ppermute | solution.py:206
  72.5 0.0 collective-permute-done.1.b_ref.refs_1_
  72.5 1.0 join.4
  73.6 4.6 %collective-permute-start.6 = (bf16[2048,256]{1,0:T(8,128)(2,1)}, bf16[2048,256]{1,0:T(8,128)(2,1)S(1)}, u32[]{:S(2)}, u32[]{:S(2)}) collective-permute-start(bf16[2048,256]{1,0:T(8,128)(2,1)} %join.4), channel_id=1, source_target_pairs={{0,1},{1,0},{2,3},{3,2},{4,5},{5,4},{6,7},{7,6},{8,9},{9,8},{10,11... | collective-permute-start | bytes 3145736 | tf_op jit(solution)/shard_map/ppermute | solution.py:206
  78.2 0.0 copy-done
  78.2 0.0 copy-done.1
  78.2 12.3 %all_to_all.10 = bf16[16,2,128]{2,1,0:T(2,128)(2,1)S(1)} all-to-all(bf16[16,2,128]{2,1,0:T(2,128)(2,1)S(1)} %broadcast_in_dim.27), channel_id=1, replica_groups=mesh['zlo'=2,'y'=8,'x'=4,'zhi'=4,'core'=2] {'zlo','zhi','core'}, dimensions={0} | all-to-all | bytes 16384 | tf_op jit(solution)/shard_map/all_to_all | solution.py:191
  90.5 0.7 broadcast_in_dim.29
  91.2 9.7 %all-to-all-start.1 = ((bf16[32,32,128]{2,1,0:T(8,128)(2,1)}), bf16[32,32,128]{2,1,0:T(8,128)(2,1)S(1)}, u32[]{:S(2)}, u32[]{:S(2)}) async-start(bf16[32,32,128]{2,1,0:T(8,128)(2,1)} %broadcast_in_dim.29), calls=%async_computation.1 | async-start | bytes 524288 | tf_op jit(solution)/shard_map/all_to_all | solution.py:191
  100.9 0.0 collective-permute-done.7.refs_3_
  100.9 2.8 %collective-permute-start.8 = (bf16[1280,256]{1,0:T(8,128)(2,1)}, bf16[1280,256]{1,0:T(8,128)(2,1)}, u32[]{:S(2)}, u32[]{:S(2)}) collective-permute-start(bf16[1280,256]{1,0:T(8,128)(2,1)} %collective-permute-done.7.refs_3_), channel_id=1, source_target_pairs={{0,1},{1,0},{2,3},{3,2},{4,5},{5,4},{6,7},{7,6},{8,9},{9,8},{10,11... | collective-permute-start | bytes 1966088 | tf_op jit(solution)/shard_map/ppermute | solution.py:206
  103.8 2.2 %collective-permute-start.2 = (bf16[768,256]{1,0:T(8,128)(2,1)S(1)}, bf16[768,256]{1,0:T(8,128)(2,1)}, u32[]{:S(2)}, u32[]{:S(2)}) collective-permute-start(bf16[768,256]{1,0:T(8,128)(2,1)S(1)} %collective-permute-done.1.b_ref.refs_1_), channel_id=1, source_target_pairs={{0,2},{2,4},{4,6},{6,0},{256,262},{258,256},{260,258},{262,260},{1... | collective-permute-start | bytes 1179656 | tf_op jit(solution)/shard_map/ppermute | solution.py:203
  106.0 2.2 %place.4 = (bf16[1024,2048]{1,0:T(8,128)(2,1)}, bf16[1024,2048]{1,0:T(8,128)(2,1)}) custom-call(bf16[2048,256]{1,0:T(8,128)(2,1)} %get-tuple-element.18.refs_0_), custom_call_target="tpu_custom_call" | custom-call | flops 1048576 | bytes 2097152 | tf_op jit(solution)/shard_map/place/pallas_call | solution.py:148
  108.2 4.0 %all-to-all-done.1 = bf16[32,32,128]{2,1,0:T(8,128)(2,1)S(1)} async-done(((bf16[32,32,128]{2,1,0:T(8,128)(2,1)}), bf16[32,32,128]{2,1,0:T(8,128)(2,1)S(1)}, u32[]{:S(2)}, u32[]{:S(2)}) %all-to-all-start.1) | async-done | bytes 262176 | tf_op jit(solution)/shard_map/all_to_all | solution.py:191
  112.2 1.0 order.1
  113.3 5.3 %collective-permute-done.2 = bf16[768,256]{1,0:T(8,128)(2,1)} collective-permute-done((bf16[768,256]{1,0:T(8,128)(2,1)S(1)}, bf16[768,256]{1,0:T(8,128)(2,1)}, u32[]{:S(2)}, u32[]{:S(2)}) %collective-permute-start.2) | collective-permute-done | bytes 393248 | tf_op jit(solution)/shard_map/ppermute | solution.py:203
  118.5 3.1 %all_gather.3.refs_0_ = bf16[1536,256]{1,0:T(8,128)(2,1)S(1)} all-gather(bf16[768,256]{1,0:T(8,128)(2,1)} %collective-permute-done.2), channel_id=1, replica_groups=mesh['zlo'=2,'y'=8,'x'=4,'zhi'=4,'core'=2] {'core'}, dimensions={0}, use_global_device_ids=true | all-gather | bytes 1179648 | tf_op jit(solution)/shard_map/all_gather | solution.py:257
  121.6 0.0 collective-permute-done.9.refs_2_
  121.6 0.0 collective-permute-done.10.refs_3_
  121.6 3.3 %place.5 = (bf16[1024,2048]{1,0:T(8,128)(2,1)}, bf16[1024,2048]{1,0:T(8,128)(2,1)}) custom-call(bf16[1280,256]{1,0:T(8,128)(2,1)S(1)} %join.3.a_ref.refs_0_, bf16[768,256]{1,0:T(8,128)(2,1)S(1)} %collective-permute-done.b_ref.refs_1_, bf16[2048,256]{1,0:T(8,128)(2,1)} %collective-permute-done.9.refs_2_, ...), custom_call_target="tpu_custom_call", output_to_operand_aliasing={{0}: (4, {}), {1}: (5, {})} | custom-call | flops 3145728 | bytes 6291456 | tf_op jit(solution)/shard_map/place/pallas_call | solution.py:148
  124.9 0.0 collective-permute-done.6.refs_2_
  124.9 0.0 collective-permute-done.8.refs_4_
  124.9 3.1 %place.6 = (bf16[1024,2048]{1,0:T(8,128)(2,1)}, bf16[1024,2048]{1,0:T(8,128)(2,1)}) custom-call(bf16[1280,256]{1,0:T(8,128)(2,1)S(1)} %collective-permute-done.5.a_ref.refs_0_, bf16[768,256]{1,0:T(8,128)(2,1)S(1)} %collective-permute-done.1.b_ref.refs_1_, ...), custom_call_target="tpu_custom_call", output_to_operand_aliasing={{0}: (5, {}), {1}: (6, {})} | custom-call | flops 3407872 | bytes 6815744 | tf_op jit(solution)/shard_map/place/pallas_call | solution.py:148
  128.0 0.9 place.7
  (3 shorter events, 0.1 us)
Async XLA Ops:
  4.1 74.0 %copy-start = (f32[256,1]{0,1:T(1,128)S(1)}, f32[256,1]{0,1:T(1,128)}, u32[]{:S(2)}) copy-start(f32[256,1]{0,1:T(1,128)} %param.12) | copy-start | bytes 3076
  4.1 74.0 %copy-start.1 = (f32[256]{0:T(256)S(1)}, f32[256]{0:T(256)}, u32[]{:S(2)}) copy-start(f32[256]{0:T(256)} %param.13) | copy-start | bytes 3076
  4.2 25.5 %collective-permute-start.4 = (bf16[768,256]{1,0:T(8,128)(2,1)S(1)}, bf16[768,256]{1,0:T(8,128)(2,1)S(1)}, u32[]{:S(2)}, u32[]{:S(2)}) collective-permute-start(bf16[768,256]{1,0:T(8,128)(2,1)S(1)} %get-tuple-element.17), channel_id=1, source_target_pairs={{0,2},{2,4},{4,6},{6,0},{256,262},{258,256},{260,258},{262,260},{1... | collective-permute-start | bytes 1179656 | tf_op jit(solution)/shard_map/ppermute | solution.py:203
  10.8 18.8 %collective-permute-start.3 = (bf16[512,256]{1,0:T(8,128)(2,1)S(1)}, bf16[512,256]{1,0:T(8,128)(2,1)S(1)}, u32[]{:S(2)}, u32[]{:S(2)}) collective-permute-start(bf16[512,256]{1,0:T(8,128)(2,1)S(1)} %mix.3.refs_4_), channel_id=1, source_target_pairs={{0,2},{2,4},{4,6},{6,0},{256,262},{258,256},{260,258},{262,260},{1... | collective-permute-start | bytes 786440 | tf_op jit(solution)/shard_map/ppermute | solution.py:203
  29.7 28.9 %collective-permute-start.5 = (bf16[1280,256]{1,0:T(8,128)(2,1)S(1)}, bf16[1280,256]{1,0:T(8,128)(2,1)S(1)}, u32[]{:S(2)}, u32[]{:S(2)}) collective-permute-start(bf16[1280,256]{1,0:T(8,128)(2,1)S(1)} %join.3.a_ref.refs_0_), channel_id=1, source_target_pairs={{0,2},{2,4},{4,6},{6,0},{256,262},{258,256},{260,258},{262,260},{1... | collective-permute-start | bytes 1966088 | tf_op jit(solution)/shard_map/ppermute | solution.py:203
  34.1 22.6 %collective-permute-start = (bf16[768,256]{1,0:T(8,128)(2,1)S(1)}, bf16[768,256]{1,0:T(8,128)(2,1)S(1)}, u32[]{:S(2)}, u32[]{:S(2)}) collective-permute-start(bf16[768,256]{1,0:T(8,128)(2,1)S(1)} %get-tuple-element.16), channel_id=1, source_target_pairs={{0,2},{2,4},{4,6},{6,0},{256,262},{258,256},{260,258},{262,260},{1... | collective-permute-start | bytes 1179656 | tf_op jit(solution)/shard_map/ppermute | solution.py:203
  56.7 15.8 %collective-permute-start.1 = (bf16[768,256]{1,0:T(8,128)(2,1)S(1)}, bf16[768,256]{1,0:T(8,128)(2,1)S(1)}, u32[]{:S(2)}, u32[]{:S(2)}) collective-permute-start(bf16[768,256]{1,0:T(8,128)(2,1)S(1)} %collective-permute-done.b_ref.refs_1_), channel_id=1, source_target_pairs={{0,2},{2,4},{4,6},{6,0},{256,262},{258,256},{260,258},{262,260},{1... | collective-permute-start | bytes 1179656 | tf_op jit(solution)/shard_map/ppermute | solution.py:203
  58.6 42.3 %collective-permute-start.7 = (bf16[1280,256]{1,0:T(8,128)(2,1)S(1)}, bf16[1280,256]{1,0:T(8,128)(2,1)}, u32[]{:S(2)}, u32[]{:S(2)}) collective-permute-start(bf16[1280,256]{1,0:T(8,128)(2,1)S(1)} %collective-permute-done.5.a_ref.refs_0_), channel_id=1, source_target_pairs={{0,2},{2,4},{4,6},{6,0},{256,262},{258,256},{260,258},{262,260},{1... | collective-permute-start | bytes 1966088 | tf_op jit(solution)/shard_map/ppermute | solution.py:203
  64.7 56.9 %collective-permute-start.9 = (bf16[2048,256]{1,0:T(8,128)(2,1)}, bf16[2048,256]{1,0:T(8,128)(2,1)}, u32[]{:S(2)}, u32[]{:S(2)}) collective-permute-start(bf16[2048,256]{1,0:T(8,128)(2,1)} %get-tuple-element.18.refs_0_), channel_id=1, source_target_pairs={{0,1},{1,0},{2,3},{3,2},{4,5},{5,4},{6,7},{7,6},{8,9},{9,8},{10,11... | collective-permute-start | bytes 3145736 | tf_op jit(solution)/shard_map/ppermute | solution.py:206
  70.6 51.0 %collective-permute-start.10 = (bf16[2048,256]{1,0:T(8,128)(2,1)}, bf16[2048,256]{1,0:T(8,128)(2,1)}, u32[]{:S(2)}, u32[]{:S(2)}) collective-permute-start(bf16[2048,256]{1,0:T(8,128)(2,1)} %join.5), channel_id=1, source_target_pairs={{0,1},{1,0},{2,3},{3,2},{4,5},{5,4},{6,7},{7,6},{8,9},{9,8},{10,11... | collective-permute-start | bytes 3145736 | tf_op jit(solution)/shard_map/ppermute | solution.py:206
  73.6 51.3 %collective-permute-start.6 = (bf16[2048,256]{1,0:T(8,128)(2,1)}, bf16[2048,256]{1,0:T(8,128)(2,1)S(1)}, u32[]{:S(2)}, u32[]{:S(2)}) collective-permute-start(bf16[2048,256]{1,0:T(8,128)(2,1)} %join.4), channel_id=1, source_target_pairs={{0,1},{1,0},{2,3},{3,2},{4,5},{5,4},{6,7},{7,6},{8,9},{9,8},{10,11... | collective-permute-start | bytes 3145736 | tf_op jit(solution)/shard_map/ppermute | solution.py:206
  91.2 21.0 %all-to-all-start.1 = ((bf16[32,32,128]{2,1,0:T(8,128)(2,1)}), bf16[32,32,128]{2,1,0:T(8,128)(2,1)S(1)}, u32[]{:S(2)}, u32[]{:S(2)}) async-start(bf16[32,32,128]{2,1,0:T(8,128)(2,1)} %broadcast_in_dim.29), calls=%async_computation.1 | async-start | bytes 524288 | tf_op jit(solution)/shard_map/all_to_all | solution.py:191
  100.9 24.0 %collective-permute-start.8 = (bf16[1280,256]{1,0:T(8,128)(2,1)}, bf16[1280,256]{1,0:T(8,128)(2,1)}, u32[]{:S(2)}, u32[]{:S(2)}) collective-permute-start(bf16[1280,256]{1,0:T(8,128)(2,1)} %collective-permute-done.7.refs_3_), channel_id=1, source_target_pairs={{0,1},{1,0},{2,3},{3,2},{4,5},{5,4},{6,7},{7,6},{8,9},{9,8},{10,11... | collective-permute-start | bytes 1966088 | tf_op jit(solution)/shard_map/ppermute | solution.py:206
  103.8 14.8 %collective-permute-start.2 = (bf16[768,256]{1,0:T(8,128)(2,1)S(1)}, bf16[768,256]{1,0:T(8,128)(2,1)}, u32[]{:S(2)}, u32[]{:S(2)}) collective-permute-start(bf16[768,256]{1,0:T(8,128)(2,1)S(1)} %collective-permute-done.1.b_ref.refs_1_), channel_id=1, source_target_pairs={{0,2},{2,4},{4,6},{6,0},{256,262},{258,256},{260,258},{262,260},{1... | collective-permute-start | bytes 1179656 | tf_op jit(solution)/shard_map/ppermute | solution.py:203
